TPU v7x, 32 devices: a whole 2x2x4 slice. The times are simulated.
32 devices in a mesh: dp: 8 (over z, y), mp: 4 (over x, core).
Axes of the slice: x: 2, y: 2, z: 4, core: 2. Of those that a mesh axis runs over, the one named last changes fastest.
Arguments:
- frames: int32 [48], P('dp'), may hold values from 17 to 129, as said below
- owners: int32 [240], P('dp'), may hold values from -1 to 7, as said below
- offsets: int32 [240], P('dp'), may hold values from -1 to 17, as said below
- groups: int32 [48], P('dp'), may hold values from 0 to 3, as said below
- latent: bfloat16 [240, 64, 128], P('dp'), may hold values from -12 to 12
- noise_blocks: bfloat16 [240, 64, 128], P('dp'), may hold values from -6 to 6
- rewards: float32 [48], P('dp'), may hold values from -6 to 6
- embed_weight: bfloat16 [64, 3072], replicated, may hold values from -2 to 2
- norm_gain: float32 [3072], replicated, may hold values from 0 to 2
- mid_weight: bfloat16 [3072, 3072], P(None, 'mp'), may hold values from -1 to 1
- head_weight: bfloat16 [3072, 64], P('mp'), may hold values from -1 to 1
Outputs:
- prediction: bfloat16 [144, 64, 128], P('dp')
- log_prob: float32 [48], P('dp')
- advantage: float32 [48], P('dp')
Inputs may be any that keep to these rules, and one draw needn't show every extreme that they name: frames = 4 m + 1 for a whole m; the block counts (frames - 1) // 32 + 1 of all samples add up to exactly 144, and some rollout device has all its samples at 129 frames. `owners`: a live slot names its owner, an empty one -1; every owner receives exactly 18 blocks; one rollout device sends at most 4 blocks to one owner, and in every draw some device sends that many to some owner. `offsets`: a live slot's row at its owner, rows distinct at each owner; empty slots -1. `groups`: every prompt has exactly 12 samples.
All inputs are finite; a program needn't handle non-finite values.
Results may differ from a plain program's by a relative error of at most 0.0068.
Values may be sent and summed in bfloat16 or wider, within the bound.
No kernel may reach another device: no remote copies, remote signals or barrier semaphores. Data moves between devices by JAX's collectives and lax.ppermute only.
A program may use at most 64 MiB of HBM per device.

v0:
```python
import functools

import jax
import jax.numpy as jnp
from jax import lax
from jax.experimental import pallas as pl
from jax.experimental.pallas import tpu as pltpu
from jax.sharding import PartitionSpec as P

GSIZE = 12
META = 16
LANES = 128
F32 = jnp.float32
BF16 = jnp.bfloat16
SMEM = pl.BlockSpec(memory_space=pltpu.SMEM)
VMEM = pl.BlockSpec(memory_space=pltpu.VMEM)
ANY = pl.BlockSpec(memory_space=pl.ANY)
HBM = pl.BlockSpec(memory_space=pltpu.HBM)


def in_hbm(value):
    return pltpu.with_memory_space_constraint(value, pltpu.HBM)


def split3(value):
    hi = value.astype(BF16)
    rest = value - hi.astype(F32)
    mid = rest.astype(BF16)
    lo = (rest - mid.astype(F32)).astype(BF16)
    return hi, mid, lo


def lane_row(scalars, count, dtype):
    lane = lax.broadcasted_iota(jnp.int32, (1, LANES), 1)
    row = jnp.zeros((1, LANES), dtype)
    for s in range(count):
        row = jnp.where(lane == s, scalars(s), row)
    return row


def live_count(frames, sample):
    return lax.shift_right_logical(frames[sample] - 1, 5) + 1


def start_kernel(
    maxb,
    per_pair,
    mp,
    step,
    frames_h,
    owners_h,
    offsets_h,
    groups_h,
    rewards_h,
    latent,
    noise,
    embed_h,
    gain_h,
    weight,
    head_h,
    out,
    gram,
    send,
    block_x,
    block_n,
    picks,
    frames,
    owners,
    offsets,
    groups,
    rewards,
    embed,
    gain,
    held,
    places,
    rows,
    chosen,
    small_sems,
    big_sems,
    weight_sems,
    row_sems,
    x_sems,
    n_sems,
):
    peers = send.shape[0]
    _, channels, width = latent.shape
    hidden = weight.shape[1]
    samples = frames.shape[0]
    share = block_x.shape[0] * 2
    small = [
        pltpu.make_async_copy(a, b, small_sems.at[n])
        for n, (a, b) in enumerate(
            [
                (frames_h, frames),
                (owners_h, owners),
                (offsets_h, offsets),
                (groups_h, groups),
                (rewards_h, rewards),
            ]
        )
    ]
    big = [
        pltpu.make_async_copy(embed_h, embed, big_sems.at[0]),
        pltpu.make_async_copy(gain_h, gain, big_sems.at[1]),
        pltpu.make_async_copy(head_h, out.at[pl.ds(channels, channels)], big_sems.at[2]),
    ]
    parts = [
        pltpu.make_async_copy(weight.at[:, pl.ds(n, step)], held.at[:, pl.ds(n, step)], weight_sems.at[n // step])
        for n in range(0, hidden, step)
    ]
    for copy in small + big + parts:
        copy.start()
    for copy in small:
        copy.wait()

    def pick(source, target, sems, i, j):
        half = pl.multiple_of(lax.rem(j, 2) * width, width)
        return pltpu.make_async_copy(source.at[i], target.at[j // 2, :, pl.ds(half, width)], sems.at[j])

    def block(o, q, i):
        return pltpu.make_async_copy(latent.at[i], send.at[o, pl.ds(q * channels, channels)], row_sems.at[o * per_pair + q])

    me = lax.axis_index("mp")
    shift = lax.rem(me + mp - lax.rem(lax.axis_index("dp"), mp), mp)
    for o in range(peers):
        places[o] = 0
        for q in range(per_pair):
            rows[o * per_pair + q] = 0
    seen = jnp.int32(0)
    count = jnp.int32(0)
    for s in range(samples):
        live_here = live_count(frames, s)
        for k in range(maxb):
            i = s * maxb + k
            live = k < live_here
            o = jnp.maximum(owners[i], 0)
            place = places[o]
            q = place // mp
            sends = live & (lax.rem(place, mp) == shift) & (q < per_pair)
            mine = live & (lax.rem(seen, mp) == me)

            @pl.when(live)
            def _():
                places[o] = place + 1

            @pl.when(sends)
            def _():
                rows[o * per_pair + q] = offsets[i] + 1
                block(o, q, i).start()

            @pl.when(mine)
            def _():
                chosen[count] = s
                pick(latent, block_x, x_sems, i, count).start()
                pick(noise, block_n, n_sems, i, count).start()

            seen = seen + live.astype(jnp.int32)
            count = count + mine.astype(jnp.int32)

    lane = lax.broadcasted_iota(jnp.int32, (1, LANES), 1)
    found = jnp.where(lane == LANES - 1, count, 0)
    for j in range(share):
        found = jnp.where((lane == j) & (j < count), chosen[j], found)
    picks[...] = found

    hi, mid, lo = split3(lane_row(lambda s: rewards[s], samples, F32))
    group = lane_row(lambda s: groups[s].astype(F32), samples, F32)
    sub = lax.broadcasted_iota(jnp.int32, (META, LANES), 0)
    shared = jnp.where(sub == 1, hi.astype(F32), 0.0)
    shared = jnp.where(sub == 2, mid.astype(F32), shared)
    shared = jnp.where(sub == 3, lo.astype(F32), shared)
    shared = jnp.where(sub == 4, group, shared)
    for o in range(peers):
        first = lane_row(lambda q: rows[o * per_pair + q].astype(F32), per_pair, F32)
        send[o, pl.ds(per_pair * channels, META), :] = jnp.where(sub == 0, first, shared).astype(BF16)

    big[0].wait()
    e = embed[...]
    hi, mid, lo = split3(lax.dot_general(e, e, (((1,), (1,)), ((), ())), preferred_element_type=F32))
    gram[...] = jnp.concatenate([hi, mid, lo], axis=0)
    big[1].wait()
    scaled = e.astype(F32) * gain[...]
    hi = scaled.astype(BF16)
    lo = (scaled - hi.astype(F32)).astype(BF16)
    both = jnp.concatenate([hi, lo], axis=0)
    for n, copy in enumerate(parts):
        copy.wait()
        m = jnp.dot(both, held[:, n * step : (n + 1) * step], preferred_element_type=F32)
        out[:channels, n * step : (n + 1) * step] = (m[:channels] + m[channels:]).astype(BF16)
    big[2].wait()
    for o in range(peers):
        for q in range(per_pair):

            @pl.when(rows[o * per_pair + q] > 0)
            def _():
                block(o, q, 0).wait()

    for j in range(share):

        @pl.when(j < count)
        def _():
            pick(latent, block_x, x_sems, 0, j).wait()
            pick(noise, block_n, n_sems, 0, j).wait()


def velocity(x, mt, heads, features):
    channels, hidden = heads[0].shape[0] // 2, heads[0].shape[1]
    tall = len(heads) * hidden
    g = jnp.dot(mt[tall:, :], x, preferred_element_type=F32)
    gx = g[:channels] + g[channels : 2 * channels] + g[2 * channels :]
    mean_sq = jnp.sum(gx * x.astype(F32), axis=0, keepdims=True) * (1.0 / features)
    half = 0.5 * lax.rsqrt(jnp.maximum(mean_sq, 0.0) + 0.25)
    step = next(n for n in (256, 128, hidden) if hidden % n == 0)
    total = None
    for m, head in enumerate(heads):
        for h in range(0, hidden, step):
            mid = jnp.dot(mt[m * hidden + h : m * hidden + h + step, :], x, preferred_element_type=F32)
            v = mid * half
            act = (v + v * jnp.tanh(v)).astype(BF16)
            part = jnp.dot(head[channels:, h : h + step], act, preferred_element_type=F32)
            total = part if total is None else total + part
    return total


def errors_kernel(shards, features, picks, block_x, block_n, gram, *refs):
    heads, (errs, mt, acc, table, sem) = refs[:shards], refs[shards:]
    channels, hidden = heads[0].shape[0] // 2, heads[0].shape[1]
    width = block_x.shape[2] // 2
    copy = pltpu.make_async_copy(picks, table, sem)
    copy.start()
    for m, head in enumerate(heads):
        mt[m * hidden : (m + 1) * hidden, :] = head[:channels, :].T
    mt[shards * hidden :, :] = gram[...]
    acc[...] = jnp.zeros_like(acc)
    copy.wait()
    count = table[0, LANES - 1]

    def body(pair, carry):
        v = velocity(block_x[pair], mt, heads, features)
        e = block_n[pair].astype(F32) + v
        rows = jnp.sum(e * e, axis=0, keepdims=True)
        acc[pl.ds(table[0, 2 * pair], 1), :] += rows[:, :width]

        @pl.when(2 * pair + 1 < count)
        def _():
            acc[pl.ds(table[0, 2 * pair + 1], 1), :] += rows[:, width:]

        return carry

    lax.fori_loop(0, (count + 1) // 2, body, 0)
    sums = jnp.sum(acc[...], axis=1, keepdims=True)
    lane = lax.broadcasted_iota(jnp.int32, acc.shape, 1)
    sub = lax.broadcasted_iota(jnp.int32, acc.shape, 0)
    errs[...] = jnp.sum(jnp.where(lane == sub, sums, 0.0), axis=0, keepdims=True)


def owner_kernel(per_pair, shards, features, recv, errs, mt, *refs):
    heads, (out, order) = refs[:shards], refs[shards:]
    peers = recv.shape[0]
    channels = heads[0].shape[0] // 2
    total = peers * per_pair
    base = total * channels
    first = recv[:, per_pair * channels, :].astype(F32)
    out[base : base + peers, :] = first.astype(BF16)
    lane = lax.broadcasted_iota(jnp.int32, (peers, LANES), 1)
    number = lax.broadcasted_iota(jnp.int32, (peers, LANES), 0) * per_pair + lane
    count = jnp.int32(0)
    for low in range(0, total, 16):
        inside = (lane < per_pair) & (number >= low) & (number < low + 16) & (first > 0)
        bits = jnp.where(inside, lax.shift_left(1, jnp.clip(number - low, 0, 15)).astype(F32), 0.0)
        mask = jnp.sum(bits).astype(jnp.int32)
        for n in range(low, min(low + 16, total)):
            live = lax.bitwise_and(lax.shift_right_logical(mask, n - low), 1)

            @pl.when(live > 0)
            def _():
                order[count] = n

            count = count + live

    def body(pair, carry):
        one = order[2 * pair]
        more = 2 * pair + 1 < count
        two = jnp.where(more, order[2 * pair + 1], one)
        x = jnp.concatenate(
            [
                recv[n // per_pair, pl.ds(pl.multiple_of((n % per_pair) * channels, channels), channels), :]
                for n in (one, two)
            ],
            axis=1,
        )
        v = velocity(x, mt, heads, features).astype(BF16)
        width = v.shape[1] // 2
        out[pl.ds(pl.multiple_of(one * channels, channels), channels), :] = v[:, :width]

        @pl.when(more)
        def _():
            out[pl.ds(pl.multiple_of(two * channels, channels), channels), :] = v[:, width:]

        return carry

    lax.fori_loop(0, (count + 1) // 2, body, 0)
    hi, mid, lo = split3(errs[...])
    sub = lax.broadcasted_iota(jnp.int32, (META, LANES), 0)
    meta = jnp.where(sub == 0, hi.astype(F32), 0.0)
    meta = jnp.where(sub == 1, mid.astype(F32), meta)
    meta = jnp.where(sub == 2, lo.astype(F32), meta)
    out[out.shape[0] - META :, :] = meta.astype(BF16)


def place_kernel(
    per_pair,
    frames_h,
    groups_h,
    rewards_h,
    recv,
    gathered,
    pred,
    log_prob,
    advantage,
    frames,
    groups,
    rewards,
    table_v,
    table,
    small_sems,
    sems,
    sem,
):
    shards = gathered.shape[0]
    channels = pred.shape[1]
    block = pred.shape[1] * pred.shape[2]
    peers = recv.shape[0]
    total = peers * per_pair
    samples = frames.shape[0]
    base = total * channels
    small = [
        pltpu.make_async_copy(a, b, small_sems.at[n])
        for n, (a, b) in enumerate([(frames_h, frames), (groups_h, groups), (rewards_h, rewards)])
    ]
    for copy in small:
        copy.start()
    for m in range(shards):
        table_v[m * peers : (m + 1) * peers, :] = gathered[m, base : base + peers, :].astype(F32).astype(jnp.int32)
    copy = pltpu.make_async_copy(table_v, table, sem)
    copy.start()
    for one in small:
        one.wait()
    copy.wait()

    def each(act):
        def body(d, carry):
            for m in range(shards):
                for q in range(per_pair):
                    row = table[m * peers + d, q]
                    n = d * per_pair + q

                    @pl.when(row > 0)
                    def _():
                        act(
                            pltpu.make_async_copy(
                                gathered.at[m, pl.ds(pl.multiple_of(n * channels, channels), channels)],
                                pred.at[row - 1],
                                sems.at[m * total + n],
                            )
                        )

            return carry

        lax.fori_loop(0, peers, body, 0, unroll=peers <= 8)

    each(lambda c: c.start())

    lane = lax.broadcasted_iota(jnp.int32, (1, LANES), 1)
    sums = jnp.zeros((1, LANES), F32)
    for m in range(shards):
        part = gathered[m, gathered.shape[1] - META :, :].astype(F32)
        sums = sums + (part[0:1] + part[1:2] + part[2:3])
    size = lane_row(lambda s: (live_count(frames, s) * block).astype(F32), samples, F32)
    logs = -0.5 * sums / jnp.where(lane < samples, size, 1.0)

    info = recv[:, pl.ds(per_pair * channels, META), :].astype(F32)
    every = info[:, 1, :] + info[:, 2, :] + info[:, 3, :]
    group = info[:, 4, :]
    inside = lax.broadcasted_iota(jnp.int32, every.shape, 1) < samples
    for s in range(samples):
        chosen = inside & (group == groups[s].astype(F32))
        mean = jnp.sum(jnp.where(chosen, every, 0.0), keepdims=True) / GSIZE
        meansq = jnp.sum(jnp.where(chosen, every * every, 0.0), keepdims=True) / GSIZE
        value = (rewards[s] - mean) / jnp.sqrt(meansq - mean * mean + 0.25)
        advantage[s] = jnp.sum(value)
        log_prob[s] = jnp.sum(jnp.where(lane == s, logs, 0.0))
    each(lambda c: c.wait())


def local(
    frames,
    owners,
    offsets,
    groups,
    latent,
    noise_blocks,
    rewards,
    embed_weight,
    norm_gain,
    mid_weight,
    head_weight,
):
    samples = frames.shape[0]
    slots, channels, width = latent.shape
    maxb = slots // samples
    peers = lax.axis_size("dp")
    mp = lax.axis_size("mp")
    features, hidden = mid_weight.shape
    pair_cap = (slots + peers - 1) // peers
    per_pair = (pair_cap + mp - 1) // mp
    total = peers * per_pair
    share = (slots + 2 * mp - 1) // (2 * mp)
    owner_rows = 3 * samples
    tall = mp * hidden + 3 * channels
    params = functools.partial(pltpu.CompilerParams, vmem_limit_bytes=48 * 1024 * 1024)
    step = next(n for n in (256, 128, hidden) if hidden % n == 0)

    combined, gram, send, block_x, block_n, picks = pl.pallas_call(
        functools.partial(start_kernel, maxb, per_pair, mp, step),
        in_specs=[HBM] * 11,
        out_specs=[VMEM] * 6,
        out_shape=[
            jax.ShapeDtypeStruct((2 * channels, hidden), BF16),
            jax.ShapeDtypeStruct((3 * channels, channels), BF16),
            pltpu.VMEM((peers, per_pair * channels + META, width), BF16),
            jax.ShapeDtypeStruct((share, channels, 2 * width), BF16),
            jax.ShapeDtypeStruct((share, channels, 2 * width), BF16),
            jax.ShapeDtypeStruct((1, LANES), jnp.int32),
        ],
        scratch_shapes=[
            pltpu.SMEM((samples,), jnp.int32),
            pltpu.SMEM((slots,), jnp.int32),
            pltpu.SMEM((slots,), jnp.int32),
            pltpu.SMEM((samples,), jnp.int32),
            pltpu.SMEM((samples,), F32),
            pltpu.VMEM((channels, features), BF16),
            pltpu.VMEM((1, features), F32),
            pltpu.VMEM((features, hidden), BF16),
            pltpu.SMEM((peers,), jnp.int32),
            pltpu.SMEM((total,), jnp.int32),
            pltpu.SMEM((2 * share,), jnp.int32),
            pltpu.SemaphoreType.DMA((5,)),
            pltpu.SemaphoreType.DMA((3,)),
            pltpu.SemaphoreType.DMA((hidden // step,)),
            pltpu.SemaphoreType.DMA((total,)),
            pltpu.SemaphoreType.DMA((2 * share,)),
            pltpu.SemaphoreType.DMA((2 * share,)),
        ],
        compiler_params=params(),
        name="start",
    )(
        *map(
            in_hbm,
            (
                frames,
                owners,
                offsets,
                groups,
                rewards,
                latent,
                noise_blocks,
                embed_weight,
                norm_gain.reshape(1, features),
                mid_weight,
                head_weight.T,
            ),
        )
    )

    paired = mp & (mp - 1) == 0
    heads = [combined]
    for s in range(mp - 1, 0, -1):
        route = [(j, j ^ s if paired else (j + s) % mp) for j in range(mp)]
        heads.append(lax.ppermute(combined, "mp", route))
    recv = lax.all_to_all(send, "dp", split_axis=0, concat_axis=0, tiled=True)

    rows8 = (samples + 7) // 8 * 8
    errs, mt = pl.pallas_call(
        functools.partial(errors_kernel, mp, features),
        in_specs=[VMEM] * (4 + mp),
        out_specs=[VMEM, VMEM],
        out_shape=[
            jax.ShapeDtypeStruct((1, LANES), F32),
            jax.ShapeDtypeStruct((tall, channels), BF16),
        ],
        scratch_shapes=[
            pltpu.VMEM((rows8, width), F32),
            pltpu.SMEM((1, LANES), jnp.int32),
            pltpu.SemaphoreType.DMA,
        ],
        compiler_params=params(),
        name="errors",
    )(picks, block_x, block_n, gram, *heads)

    tail = (peers + META - 1) // META * META + META
    payload = pl.pallas_call(
        functools.partial(owner_kernel, per_pair, mp, features),
        in_specs=[VMEM] * (3 + mp),
        out_specs=VMEM,
        out_shape=jax.ShapeDtypeStruct((total * channels + tail, width), BF16),
        scratch_shapes=[pltpu.SMEM((total,), jnp.int32)],
        compiler_params=params(),
        name="owner",
    )(recv, errs, mt, *heads)

    gathered = lax.all_gather(payload, "mp", axis=0, tiled=False)

    return pl.pallas_call(
        functools.partial(place_kernel, per_pair),
        in_specs=[HBM] * 3 + [VMEM, VMEM],
        out_specs=[ANY, SMEM, SMEM],
        out_shape=[
            jax.ShapeDtypeStruct((owner_rows, channels, width), BF16),
            jax.ShapeDtypeStruct((samples,), F32),
            jax.ShapeDtypeStruct((samples,), F32),
        ],
        scratch_shapes=[
            pltpu.SMEM((samples,), jnp.int32),
            pltpu.SMEM((samples,), jnp.int32),
            pltpu.SMEM((samples,), F32),
            pltpu.VMEM((mp * peers, LANES), jnp.int32),
            pltpu.SMEM((mp * peers, LANES), jnp.int32),
            pltpu.SemaphoreType.DMA((3,)),
            pltpu.SemaphoreType.DMA((mp * total,)),
            pltpu.SemaphoreType.DMA,
        ],
        compiler_params=params(),
        name="place",
    )(in_hbm(frames), in_hbm(groups), in_hbm(rewards), recv, gathered)


def solution(mesh):
    placed = (
        P("dp"),
        P("dp"),
        P("dp"),
        P("dp"),
        P("dp", None, None),
        P("dp", None, None),
        P("dp"),
        P(),
        P(),
        P(None, "mp"),
        P("mp", None),
    )
    return jax.shard_map(
        local,
        mesh=mesh,
        in_specs=placed,
        out_specs=(P("dp", None, None), P("dp"), P("dp")),
        check_vma=False,
    )
```

profile of v0, /device:TPU:13, one launch (start us, length us, event | category | flops | bytes accessed | tf_op | source)
XLA Modules:
  0.0 43.9 jit_solution(9539467460136740514)
XLA Ops:
  0.6 4.7 %start.1 = (bf16[128,768]{1,0:T(8,128)(2,1)S(1)}, bf16[192,64]{1,0:T(8,128)(2,1)S(1)}, bf16[8,80,128]{2,1,0:T(8,128)(2,1)}, bf16[4,64,256]{2,1,0:T(8,128)(2,1)S(...) custom-call(s32[6]{0:T(128)} %frames_h.3, s32[30]{0:T(128)} %owners_h.1, s32[30]{0:T(128)} %offsets_h.1, ...), custom_call_target="tpu_custom_call" | custom-call | tf_op jit(solution)/shard_map/start/pallas_call | solution.py:424
  5.4 5.7 %all-to-all-start = ((bf16[8,80,128]{2,1,0:T(8,128)(2,1)}), bf16[8,80,128]{2,1,0:T(8,128)(2,1)S(1)}, u32[]{:S(2)}, u32[]{:S(2)}) async-start(bf16[8,80,128]{2,1,0:T(8,128)(2,1)} %get-tuple-element.11), calls=%async_computation | async-start | bytes 327680 | tf_op jit(solution)/shard_map/all_to_all | solution.py:481
  11.0 1.2 %collective-permute-start.2 = (bf16[128,768]{1,0:T(8,128)(2,1)S(1)}, bf16[128,768]{1,0:T(8,128)(2,1)S(1)}, u32[]{:S(2)}, u32[]{:S(2)}) collective-permute-start(bf16[128,768]{1,0:T(8,128)(2,1)S(1)} %get-tuple-element.16.refs_0_), channel_id=1, source_target_pairs={{0,1},{1,0},{2,3},{3,2},{4,5},{5,4},{6,7},{7,6},{8,9},{9,8},{10,11... | collective-permute-start | bytes 589832 | tf_op jit(solution)/shard_map/ppermute | solution.py:480
  12.3 1.2 %collective-permute-start.1 = (bf16[128,768]{1,0:T(8,128)(2,1)S(1)}, bf16[128,768]{1,0:T(8,128)(2,1)S(1)}, u32[]{:S(2)}, u32[]{:S(2)}) collective-permute-start(bf16[128,768]{1,0:T(8,128)(2,1)S(1)} %get-tuple-element.16.refs_0_), channel_id=1, source_target_pairs={{0,2},{1,3},{2,0},{3,1},{4,6},{5,7},{6,4},{7,5},{8,10},{9,11},{10,... | collective-permute-start | bytes 589832 | tf_op jit(solution)/shard_map/ppermute | solution.py:480
  13.5 0.4 collective-permute-start
  13.9 0.0 collective-permute-done.2.refs_3_
  13.9 4.8 %collective-permute-done.1.refs_2_ = bf16[128,768]{1,0:T(8,128)(2,1)S(1)} collective-permute-done((bf16[128,768]{1,0:T(8,128)(2,1)S(1)}, bf16[128,768]{1,0:T(8,128)(2,1)S(1)}, u32[]{:S(2)}, u32[]{:S(2)}) %collective-permute-start.1) | collective-permute-done | bytes 196640 | tf_op jit(solution)/shard_map/ppermute | solution.py:480
  18.7 4.4 %collective-permute-done.refs_1_ = bf16[128,768]{1,0:T(8,128)(2,1)S(1)} collective-permute-done((bf16[128,768]{1,0:T(8,128)(2,1)S(1)}, bf16[128,768]{1,0:T(8,128)(2,1)S(1)}, u32[]{:S(2)}, u32[]{:S(2)}) %collective-permute-start) | collective-permute-done | bytes 196640 | tf_op jit(solution)/shard_map/ppermute | solution.py:480
  23.1 6.3 %errors.1 = (f32[1,128]{1,0:T(1,128)S(1)}, bf16[3264,64]{1,0:T(8,128)(2,1)S(1)}) custom-call(s32[1,128]{1,0:T(1,128)S(1)} %get-tuple-element.12.picks, bf16[4,64,256]{2,1,0:T(8,128)(2,1)S(1)} %get-tuple-element.13.block_x, bf16[4,64,256]{2,1,0:T(8,128)(2,1)S(1)} %get-tuple-element.14.block_n, bf16[192,64]{1,0:T(8,128)(2,1)S(1)} %get-tuple-element.15.gram, ...), custom_call_target="tpu_custom_call" | custom-call | tf_op jit(solution)/shard_map/errors/pallas_call | solution.py:484
  29.4 0.0 all-to-all-done.recv
  29.4 4.4 %owner.1 = bf16[544,128]{1,0:T(8,128)(2,1)S(1)} custom-call(bf16[8,80,128]{2,1,0:T(8,128)(2,1)S(1)} %all-to-all-done.recv, f32[1,128]{1,0:T(1,128)S(1)} %get-tuple-element.17.errs, bf16[3264,64]{1,0:T(8,128)(2,1)S(1)} %get-tuple-element.18.mt, bf16[128,768]{1,0:T(8,128)(2,1)S(1)} %get-tuple-element.16.refs_0_, ...), custom_call_target="tpu_custom_call" | custom-call | tf_op jit(solution)/shard_map/owner/pallas_call | solution.py:502
  33.8 7.5 %all-gather = bf16[2176,128]{1,0:T(8,128)(2,1)S(1)} all-gather(bf16[544,128]{1,0:T(8,128)(2,1)S(1)} %owner.1), channel_id=2, replica_groups=mesh['dp'=8,'mp'=4] {'mp'}, dimensions={0}, use_global_device_ids=true | all-gather | bytes 696320 | tf_op jit(solution)/shard_map/all_gather | solution.py:512
  41.2 2.7 %place.1 = (bf16[18,64,128]{2,1,0:T(8,128)(2,1)}, f32[6]{0:T(128)}, f32[6]{0:T(128)}) custom-call(s32[6]{0:T(128)} %frames_h.3, s32[6]{0:T(128)} %groups_h.3, f32[6]{0:T(128)} %rewards_h.3, bf16[8,80,128]{2,1,0:T(8,128)(2,1)S(1)} %all-to-all-done.recv, bf16[4,544,128]{2,1,0:T(8,128)(2,1)S(1)} %bitcast.3), custom_call_target="tpu_custom_call" | custom-call | tf_op jit(solution)/shard_map/place/pallas_call | solution.py:514
Async XLA Ops:
  5.4 24.0 %all-to-all-start = ((bf16[8,80,128]{2,1,0:T(8,128)(2,1)}), bf16[8,80,128]{2,1,0:T(8,128)(2,1)S(1)}, u32[]{:S(2)}, u32[]{:S(2)}) async-start(bf16[8,80,128]{2,1,0:T(8,128)(2,1)} %get-tuple-element.11), calls=%async_computation | async-start | bytes 327680 | tf_op jit(solution)/shard_map/all_to_all | solution.py:481
  11.0 2.9 %collective-permute-start.2 = (bf16[128,768]{1,0:T(8,128)(2,1)S(1)}, bf16[128,768]{1,0:T(8,128)(2,1)S(1)}, u32[]{:S(2)}, u32[]{:S(2)}) collective-permute-start(bf16[128,768]{1,0:T(8,128)(2,1)S(1)} %get-tuple-element.16.refs_0_), channel_id=1, source_target_pairs={{0,1},{1,0},{2,3},{3,2},{4,5},{5,4},{6,7},{7,6},{8,9},{9,8},{10,11... | collective-permute-start | bytes 589832 | tf_op jit(solution)/shard_map/ppermute | solution.py:480
  12.3 6.5 %collective-permute-start.1 = (bf16[128,768]{1,0:T(8,128)(2,1)S(1)}, bf16[128,768]{1,0:T(8,128)(2,1)S(1)}, u32[]{:S(2)}, u32[]{:S(2)}) collective-permute-start(bf16[128,768]{1,0:T(8,128)(2,1)S(1)} %get-tuple-element.16.refs_0_), channel_id=1, source_target_pairs={{0,2},{1,3},{2,0},{3,1},{4,6},{5,7},{6,4},{7,5},{8,10},{9,11},{10,... | collective-permute-start | bytes 589832 | tf_op jit(solution)/shard_map/ppermute | solution.py:480
  13.5 9.6 %collective-permute-start = (bf16[128,768]{1,0:T(8,128)(2,1)S(1)}, bf16[128,768]{1,0:T(8,128)(2,1)S(1)}, u32[]{:S(2)}, u32[]{:S(2)}) collective-permute-start(bf16[128,768]{1,0:T(8,128)(2,1)S(1)} %get-tuple-element.16.refs_0_), channel_id=1, source_target_pairs={{0,3},{1,2},{2,1},{3,0},{4,7},{5,6},{6,5},{7,4},{8,11},{9,10},{10,... | collective-permute-start | bytes 589832 | tf_op jit(solution)/shard_map/ppermute | solution.py:480
where the time goes:
time: 44.1 us; the launch traced here: 43.9 us
  Pallas kernels  18 us (41%)
  waiting for transfers between devices  9.21 us (21%)
  starting transfers between devices  8.54 us (19%)
  blocking collectives  7.46 us (17%)
  between operations  0.67 us (2%)
    ppermute x3, waiting for transfers between devices, local(): heads.append(lax.ppermute(combined, 'mp', route))  9.2 us
    all_gather x1, blocking collectives, local(): gathered = lax.all_gather(payload, 'mp', axis=0, tiled=False)  7.46 us
    pallas_call x1, Pallas kernels, local(): pl.pallas_call(functools.partial(errors_kernel, mp, features), in_specs=[...  6.27 us
    all_to_all x1, starting transfers between devices, local(): recv = lax.all_to_all(send, 'dp', split_axis=0, concat_axis=0, tiled=True)  5.67 us
    pallas_call x1, Pallas kernels, local(): pl.pallas_call(functools.partial(start_kernel, maxb, per_pair, mp, step),...  4.72 us
    pallas_call x1, Pallas kernels, local(): pl.pallas_call(functools.partial(owner_kernel, per_pair, mp, features), i...  4.35 us
    ppermute x3, starting transfers between devices, local(): heads.append(lax.ppermute(combined, 'mp', route))  2.87 us
    pallas_call x1, Pallas kernels, local(): pl.pallas_call(functools.partial(place_kernel, per_pair), in_specs=[HBM]...  2.7 us
  transfers between devices with their start and end apart: 4, of which 2 were waited for; matrix products, arithmetic and copies ran while one was open for 0% of the time, Pallas kernels for 14%

commit v1 on v0

--- a/solution.py
+++ b/solution.py
@@ -40,6 +40,14 @@
 
 def live_count(frames, sample):
     return lax.shift_right_logical(frames[sample] - 1, 5) + 1
+
+
+def rest_of(value, mp):
+    return lax.bitwise_and(value, mp - 1) if mp & (mp - 1) == 0 else lax.rem(value, mp)
+
+
+def part_of(value, mp):
+    return lax.shift_right_logical(value, mp.bit_length() - 1) if mp & (mp - 1) == 0 else value // mp
 
 
 def start_kernel(
@@ -74,7 +82,9 @@
     held,
     places,
     rows,
+    source,
     chosen,
+    slot_of,
     small_sems,
     big_sems,
     weight_sems,
@@ -87,6 +97,7 @@
     hidden = weight.shape[1]
     samples = frames.shape[0]
     share = block_x.shape[0] * 2
+    total = peers * per_pair
     small = [
         pltpu.make_async_copy(a, b, small_sems.at[n])
         for n, (a, b) in enumerate(
@@ -108,24 +119,21 @@
         pltpu.make_async_copy(weight.at[:, pl.ds(n, step)], held.at[:, pl.ds(n, step)], weight_sems.at[n // step])
         for n in range(0, hidden, step)
     ]
-    for copy in small + big + parts:
+    for copy in small + big[:2] + parts + big[2:]:
         copy.start()
+
+    me = lax.axis_index("mp")
+    shift = rest_of(me + mp - rest_of(lax.axis_index("dp"), mp), mp)
+    for o in range(peers + 1):
+        places[o] = 0
+    for n in range(total + 1):
+        rows[n] = 0
+        source[n] = 0
+    for j in range(share + 1):
+        chosen[j] = 0
+        slot_of[j] = 0
     for copy in small:
         copy.wait()
-
-    def pick(source, target, sems, i, j):
-        half = pl.multiple_of(lax.rem(j, 2) * width, width)
-        return pltpu.make_async_copy(source.at[i], target.at[j // 2, :, pl.ds(half, width)], sems.at[j])
-
-    def block(o, q, i):
-        return pltpu.make_async_copy(latent.at[i], send.at[o, pl.ds(q * channels, channels)], row_sems.at[o * per_pair + q])
-
-    me = lax.axis_index("mp")
-    shift = lax.rem(me + mp - lax.rem(lax.axis_index("dp"), mp), mp)
-    for o in range(peers):
-        places[o] = 0
-        for q in range(per_pair):
-            rows[o * per_pair + q] = 0
     seen = jnp.int32(0)
     count = jnp.int32(0)
     for s in range(samples):
@@ -133,34 +141,40 @@
         for k in range(maxb):
             i = s * maxb + k
             live = k < live_here
-            o = jnp.maximum(owners[i], 0)
+            o = jnp.where(live, owners[i], peers)
             place = places[o]
-            q = place // mp
-            sends = live & (lax.rem(place, mp) == shift) & (q < per_pair)
-            mine = live & (lax.rem(seen, mp) == me)
-
-            @pl.when(live)
-            def _():
-                places[o] = place + 1
-
-            @pl.when(sends)
-            def _():
-                rows[o * per_pair + q] = offsets[i] + 1
-                block(o, q, i).start()
-
-            @pl.when(mine)
-            def _():
-                chosen[count] = s
-                pick(latent, block_x, x_sems, i, count).start()
-                pick(noise, block_n, n_sems, i, count).start()
-
+            places[o] = place + 1
+            q = part_of(place, mp)
+            sends = live & (rest_of(place, mp) == shift) & (q < per_pair)
+            n = jnp.where(sends, o * per_pair + q, total)
+            rows[n] = offsets[i] + 1
+            source[n] = i
+            chosen[count] = s
+            slot_of[count] = i
+            mine = live & (rest_of(seen, mp) == me)
             seen = seen + live.astype(jnp.int32)
             count = count + mine.astype(jnp.int32)
+
+    copies = [
+        pltpu.make_async_copy(
+            latent.at[source[o * per_pair + q]],
+            send.at[o, pl.ds(q * channels, channels)],
+            row_sems.at[o * per_pair + q],
+        )
+        for o in range(peers)
+        for q in range(per_pair)
+    ]
+    for j in range(share):
+        lanes = pl.ds(j % 2 * width, width)
+        copies.append(pltpu.make_async_copy(latent.at[slot_of[j]], block_x.at[j // 2, :, lanes], x_sems.at[j]))
+        copies.append(pltpu.make_async_copy(noise.at[slot_of[j]], block_n.at[j // 2, :, lanes], n_sems.at[j]))
+    for copy in copies:
+        copy.start()
 
     lane = lax.broadcasted_iota(jnp.int32, (1, LANES), 1)
     found = jnp.where(lane == LANES - 1, count, 0)
     for j in range(share):
-        found = jnp.where((lane == j) & (j < count), chosen[j], found)
+        found = jnp.where(lane == j, chosen[j], found)
     picks[...] = found
 
     hi, mid, lo = split3(lane_row(lambda s: rewards[s], samples, F32))
@@ -176,8 +190,6 @@
 
     big[0].wait()
     e = embed[...]
-    hi, mid, lo = split3(lax.dot_general(e, e, (((1,), (1,)), ((), ())), preferred_element_type=F32))
-    gram[...] = jnp.concatenate([hi, mid, lo], axis=0)
     big[1].wait()
     scaled = e.astype(F32) * gain[...]
     hi = scaled.astype(BF16)
@@ -187,56 +199,68 @@
         copy.wait()
         m = jnp.dot(both, held[:, n * step : (n + 1) * step], preferred_element_type=F32)
         out[:channels, n * step : (n + 1) * step] = (m[:channels] + m[channels:]).astype(BF16)
+    hi, mid, lo = split3(lax.dot_general(e, e, (((1,), (1,)), ((), ())), preferred_element_type=F32))
+    gram[...] = jnp.concatenate([hi, mid, lo], axis=0)
     big[2].wait()
-    for o in range(peers):
-        for q in range(per_pair):
-
-            @pl.when(rows[o * per_pair + q] > 0)
-            def _():
-                block(o, q, 0).wait()
-
-    for j in range(share):
-
-        @pl.when(j < count)
-        def _():
-            pick(latent, block_x, x_sems, 0, j).wait()
-            pick(noise, block_n, n_sems, 0, j).wait()
-
-
-def velocity(x, mt, heads, features):
-    channels, hidden = heads[0].shape[0] // 2, heads[0].shape[1]
-    tall = len(heads) * hidden
-    g = jnp.dot(mt[tall:, :], x, preferred_element_type=F32)
+    for copy in copies:
+        copy.wait()
+
+
+def norm_factor(x, gram, features):
+    channels = x.shape[0]
+    g = jnp.dot(gram, x, preferred_element_type=F32)
     gx = g[:channels] + g[channels : 2 * channels] + g[2 * channels :]
     mean_sq = jnp.sum(gx * x.astype(F32), axis=0, keepdims=True) * (1.0 / features)
-    half = 0.5 * lax.rsqrt(jnp.maximum(mean_sq, 0.0) + 0.25)
-    step = next(n for n in (256, 128, hidden) if hidden % n == 0)
-    total = None
+    return 0.5 * lax.rsqrt(jnp.maximum(mean_sq, 0.0) + 0.25)
+
+
+def velocity(x, half, mt, heads, total=None):
+    channels, hidden = heads[0].shape[0] // 2, heads[0].shape[1]
     for m, head in enumerate(heads):
-        for h in range(0, hidden, step):
-            mid = jnp.dot(mt[m * hidden + h : m * hidden + h + step, :], x, preferred_element_type=F32)
-            v = mid * half
-            act = (v + v * jnp.tanh(v)).astype(BF16)
-            part = jnp.dot(head[channels:, h : h + step], act, preferred_element_type=F32)
-            total = part if total is None else total + part
+        mid = jnp.dot(mt[m * hidden : (m + 1) * hidden, :], x, preferred_element_type=F32)
+        v = mid * half
+        act = (v + v * jnp.tanh(v)).astype(BF16)
+        part = jnp.dot(head[channels:, :], act, preferred_element_type=F32)
+        total = part if total is None else total + part
     return total
 
 
-def errors_kernel(shards, features, picks, block_x, block_n, gram, *refs):
-    heads, (errs, mt, acc, table, sem) = refs[:shards], refs[shards:]
+def turn(mt, heads):
     channels, hidden = heads[0].shape[0] // 2, heads[0].shape[1]
+    for m, head in enumerate(heads):
+        mt[m * hidden : (m + 1) * hidden, :] = head[:channels, :].T
+
+
+def early_kernel(near, features, picks, block_x, gram, *refs):
+    heads, (partial, halves, mt, table, sem) = refs[:near], refs[near:]
+    copy = pltpu.make_async_copy(picks, table, sem)
+    copy.start()
+    turn(mt, heads)
+    copy.wait()
+    count = table[0, LANES - 1]
+
+    def body(pair, carry):
+        x = block_x[pair]
+        half = norm_factor(x, gram[...], features)
+        halves[pair] = half
+        partial[pair] = velocity(x, half, mt, heads)
+        return carry
+
+    lax.fori_loop(0, (count + 1) // 2, body, 0)
+
+
+def errors_kernel(far, picks, block_x, block_n, partial, halves, *refs):
+    heads, (errs, mt, acc, table, sem) = refs[:far], refs[far:]
     width = block_x.shape[2] // 2
     copy = pltpu.make_async_copy(picks, table, sem)
     copy.start()
-    for m, head in enumerate(heads):
-        mt[m * hidden : (m + 1) * hidden, :] = head[:channels, :].T
-    mt[shards * hidden :, :] = gram[...]
+    turn(mt, heads)
     acc[...] = jnp.zeros_like(acc)
     copy.wait()
     count = table[0, LANES - 1]
 
     def body(pair, carry):
-        v = velocity(block_x[pair], mt, heads, features)
+        v = velocity(block_x[pair], halves[pair], mt, heads, partial[pair])
         e = block_n[pair].astype(F32) + v
         rows = jnp.sum(e * e, axis=0, keepdims=True)
         acc[pl.ds(table[0, 2 * pair], 1), :] += rows[:, :width]
@@ -254,7 +278,7 @@
     errs[...] = jnp.sum(jnp.where(lane == sub, sums, 0.0), axis=0, keepdims=True)
 
 
-def owner_kernel(per_pair, shards, features, recv, errs, mt, *refs):
+def owner_kernel(per_pair, near, shards, features, recv, errs, gram, mt_near, mt_far, *refs):
     heads, (out, order) = refs[:shards], refs[shards:]
     peers = recv.shape[0]
     channels = heads[0].shape[0] // 2
@@ -262,6 +286,12 @@
     base = total * channels
     first = recv[:, per_pair * channels, :].astype(F32)
     out[base : base + peers, :] = first.astype(BF16)
+    hi, mid, lo = split3(errs[...])
+    sub = lax.broadcasted_iota(jnp.int32, (META, LANES), 0)
+    meta = jnp.where(sub == 0, hi.astype(F32), 0.0)
+    meta = jnp.where(sub == 1, mid.astype(F32), meta)
+    meta = jnp.where(sub == 2, lo.astype(F32), meta)
+    out[out.shape[0] - META :, :] = meta.astype(BF16)
     lane = lax.broadcasted_iota(jnp.int32, (peers, LANES), 1)
     number = lax.broadcasted_iota(jnp.int32, (peers, LANES), 0) * per_pair + lane
     count = jnp.int32(0)
@@ -270,13 +300,8 @@
         bits = jnp.where(inside, lax.shift_left(1, jnp.clip(number - low, 0, 15)).astype(F32), 0.0)
         mask = jnp.sum(bits).astype(jnp.int32)
         for n in range(low, min(low + 16, total)):
-            live = lax.bitwise_and(lax.shift_right_logical(mask, n - low), 1)
-
-            @pl.when(live > 0)
-            def _():
-                order[count] = n
-
-            count = count + live
+            order[count] = n
+            count = count + lax.bitwise_and(lax.shift_right_logical(mask, n - low), 1)
 
     def body(pair, carry):
         one = order[2 * pair]
@@ -289,7 +314,9 @@
             ],
             axis=1,
         )
-        v = velocity(x, mt, heads, features).astype(BF16)
+        half = norm_factor(x, gram[...], features)
+        v = velocity(x, half, mt_near, heads[:near])
+        v = velocity(x, half, mt_far, heads[near:], v).astype(BF16)
         width = v.shape[1] // 2
         out[pl.ds(pl.multiple_of(one * channels, channels), channels), :] = v[:, :width]
 
@@ -300,12 +327,6 @@
         return carry
 
     lax.fori_loop(0, (count + 1) // 2, body, 0)
-    hi, mid, lo = split3(errs[...])
-    sub = lax.broadcasted_iota(jnp.int32, (META, LANES), 0)
-    meta = jnp.where(sub == 0, hi.astype(F32), 0.0)
-    meta = jnp.where(sub == 1, mid.astype(F32), meta)
-    meta = jnp.where(sub == 2, lo.astype(F32), meta)
-    out[out.shape[0] - META :, :] = meta.astype(BF16)
 
 
 def place_kernel(
@@ -316,20 +337,18 @@
     recv,
     gathered,
     pred,
-    log_prob,
-    advantage,
+    log_out,
+    adv_out,
     frames,
     groups,
     rewards,
-    table_v,
-    table,
+    log_prob,
+    advantage,
     small_sems,
-    sems,
     sem,
 ):
     shards = gathered.shape[0]
-    channels = pred.shape[1]
-    block = pred.shape[1] * pred.shape[2]
+    rows_here, channels, width = pred.shape
     peers = recv.shape[0]
     total = peers * per_pair
     samples = frames.shape[0]
@@ -340,43 +359,33 @@
     ]
     for copy in small:
         copy.start()
+    bits = rows_here.bit_length()
+    pack = 24 // bits
+    lane8 = lax.broadcasted_iota(jnp.int32, (peers, LANES), 1)
+    number = lax.broadcasted_iota(jnp.int32, (peers, LANES), 0) * per_pair + lane8
+    scale = lax.shift_left(1, bits * lax.rem(number, pack)).astype(F32)
     for m in range(shards):
-        table_v[m * peers : (m + 1) * peers, :] = gathered[m, base : base + peers, :].astype(F32).astype(jnp.int32)
-    copy = pltpu.make_async_copy(table_v, table, sem)
-    copy.start()
-    for one in small:
-        one.wait()
-    copy.wait()
-
-    def each(act):
-        def body(d, carry):
-            for m in range(shards):
-                for q in range(per_pair):
-                    row = table[m * peers + d, q]
-                    n = d * per_pair + q
-
-                    @pl.when(row > 0)
-                    def _():
-                        act(
-                            pltpu.make_async_copy(
-                                gathered.at[m, pl.ds(pl.multiple_of(n * channels, channels), channels)],
-                                pred.at[row - 1],
-                                sems.at[m * total + n],
-                            )
-                        )
-
-            return carry
-
-        lax.fori_loop(0, peers, body, 0, unroll=peers <= 8)
-
-    each(lambda c: c.start())
-
+        first = gathered[m, base : base + peers, :].astype(F32)
+        for low in range(0, total, pack):
+            inside = (lane8 < per_pair) & (number >= low) & (number < low + pack)
+            code = jnp.sum(jnp.where(inside, first * scale, 0.0)).astype(jnp.int32)
+            for n in range(low, min(low + pack, total)):
+                row = lax.bitwise_and(lax.shift_right_logical(code, bits * (n - low)), 2**bits - 1)
+
+                @pl.when(row > 0)
+                def _():
+                    pltpu.make_async_copy(
+                        gathered.at[m, pl.ds(n * channels, channels)], pred.at[row - 1], sem
+                    ).start()
+
+    for copy in small:
+        copy.wait()
     lane = lax.broadcasted_iota(jnp.int32, (1, LANES), 1)
     sums = jnp.zeros((1, LANES), F32)
     for m in range(shards):
         part = gathered[m, gathered.shape[1] - META :, :].astype(F32)
         sums = sums + (part[0:1] + part[1:2] + part[2:3])
-    size = lane_row(lambda s: (live_count(frames, s) * block).astype(F32), samples, F32)
+    size = lane_row(lambda s: (live_count(frames, s) * (channels * width)).astype(F32), samples, F32)
     logs = -0.5 * sums / jnp.where(lane < samples, size, 1.0)
 
     info = recv[:, pl.ds(per_pair * channels, META), :].astype(F32)
@@ -390,7 +399,15 @@
         value = (rewards[s] - mean) / jnp.sqrt(meansq - mean * mean + 0.25)
         advantage[s] = jnp.sum(value)
         log_prob[s] = jnp.sum(jnp.where(lane == s, logs, 0.0))
-    each(lambda c: c.wait())
+    last = [
+        pltpu.make_async_copy(log_prob, log_out, small_sems.at[0]),
+        pltpu.make_async_copy(advantage, adv_out, small_sems.at[1]),
+    ]
+    for copy in last:
+        copy.start()
+    pltpu.make_async_copy(pred, pred, sem).wait()
+    for copy in last:
+        copy.wait()
 
 
 def local(
@@ -417,7 +434,6 @@
     total = peers * per_pair
     share = (slots + 2 * mp - 1) // (2 * mp)
     owner_rows = 3 * samples
-    tall = mp * hidden + 3 * channels
     params = functools.partial(pltpu.CompilerParams, vmem_limit_bytes=48 * 1024 * 1024)
     step = next(n for n in (256, 128, hidden) if hidden % n == 0)
 
@@ -442,9 +458,11 @@
             pltpu.VMEM((channels, features), BF16),
             pltpu.VMEM((1, features), F32),
             pltpu.VMEM((features, hidden), BF16),
-            pltpu.SMEM((peers,), jnp.int32),
-            pltpu.SMEM((total,), jnp.int32),
-            pltpu.SMEM((2 * share,), jnp.int32),
+            pltpu.SMEM((peers + 1,), jnp.int32),
+            pltpu.SMEM((total + 1,), jnp.int32),
+            pltpu.SMEM((total + 1,), jnp.int32),
+            pltpu.SMEM((2 * share + 1,), jnp.int32),
+            pltpu.SMEM((2 * share + 1,), jnp.int32),
             pltpu.SemaphoreType.DMA((5,)),
             pltpu.SemaphoreType.DMA((3,)),
             pltpu.SemaphoreType.DMA((hidden // step,)),
@@ -474,20 +492,35 @@
     )
 
     paired = mp & (mp - 1) == 0
+    near = max(mp // 2, 1)
     heads = [combined]
-    for s in range(mp - 1, 0, -1):
+    for s in range(1, mp):
         route = [(j, j ^ s if paired else (j + s) % mp) for j in range(mp)]
         heads.append(lax.ppermute(combined, "mp", route))
     recv = lax.all_to_all(send, "dp", split_axis=0, concat_axis=0, tiled=True)
 
+    partial, halves, mt_near = pl.pallas_call(
+        functools.partial(early_kernel, near, features),
+        in_specs=[VMEM] * (3 + near),
+        out_specs=[VMEM] * 3,
+        out_shape=[
+            jax.ShapeDtypeStruct((share, channels, 2 * width), F32),
+            jax.ShapeDtypeStruct((share, 1, 2 * width), F32),
+            jax.ShapeDtypeStruct((near * hidden, channels), BF16),
+        ],
+        scratch_shapes=[pltpu.SMEM((1, LANES), jnp.int32), pltpu.SemaphoreType.DMA],
+        compiler_params=params(),
+        name="early",
+    )(picks, block_x, gram, *heads[:near])
+
     rows8 = (samples + 7) // 8 * 8
-    errs, mt = pl.pallas_call(
-        functools.partial(errors_kernel, mp, features),
-        in_specs=[VMEM] * (4 + mp),
+    errs, mt_far = pl.pallas_call(
+        functools.partial(errors_kernel, mp - near),
+        in_specs=[VMEM] * (5 + mp - near),
         out_specs=[VMEM, VMEM],
         out_shape=[
             jax.ShapeDtypeStruct((1, LANES), F32),
-            jax.ShapeDtypeStruct((tall, channels), BF16),
+            jax.ShapeDtypeStruct(((mp - near) * hidden, channels), BF16),
         ],
         scratch_shapes=[
             pltpu.VMEM((rows8, width), F32),
@@ -496,25 +529,25 @@
         ],
         compiler_params=params(),
         name="errors",
-    )(picks, block_x, block_n, gram, *heads)
+    )(picks, block_x, block_n, partial, halves, *heads[near:])
 
     tail = (peers + META - 1) // META * META + META
     payload = pl.pallas_call(
-        functools.partial(owner_kernel, per_pair, mp, features),
-        in_specs=[VMEM] * (3 + mp),
+        functools.partial(owner_kernel, per_pair, near, mp, features),
+        in_specs=[VMEM] * (5 + mp),
         out_specs=VMEM,
         out_shape=jax.ShapeDtypeStruct((total * channels + tail, width), BF16),
-        scratch_shapes=[pltpu.SMEM((total,), jnp.int32)],
+        scratch_shapes=[pltpu.SMEM((total + 1,), jnp.int32)],
         compiler_params=params(),
         name="owner",
-    )(recv, errs, mt, *heads)
+    )(recv, errs, gram, mt_near, mt_far, *heads)
 
     gathered = lax.all_gather(payload, "mp", axis=0, tiled=False)
 
     return pl.pallas_call(
         functools.partial(place_kernel, per_pair),
         in_specs=[HBM] * 3 + [VMEM, VMEM],
-        out_specs=[ANY, SMEM, SMEM],
+        out_specs=[ANY] * 3,
         out_shape=[
             jax.ShapeDtypeStruct((owner_rows, channels, width), BF16),
             jax.ShapeDtypeStruct((samples,), F32),
@@ -524,10 +557,9 @@
             pltpu.SMEM((samples,), jnp.int32),
             pltpu.SMEM((samples,), jnp.int32),
             pltpu.SMEM((samples,), F32),
-            pltpu.VMEM((mp * peers, LANES), jnp.int32),
-            pltpu.SMEM((mp * peers, LANES), jnp.int32),
+            pltpu.SMEM((samples,), F32),
+            pltpu.SMEM((samples,), F32),
             pltpu.SemaphoreType.DMA((3,)),
-            pltpu.SemaphoreType.DMA((mp * total,)),
             pltpu.SemaphoreType.DMA,
         ],
         compiler_params=params(),

time: 44.1 us -> 39.5 us (0.90)
  the two profiles are of different devices: /device:TPU:13 before, /device:TPU:0 now
where the time goes in v1:
time: 39.5 us; the launch traced here: 39.2 us
  Pallas kernels  14.1 us (36%)
  starting transfers between devices  9.46 us (24%)
  blocking collectives  8.41 us (21%)
  waiting for transfers between devices  6.54 us (17%)
  between operations  0.68 us (2%)
    all_gather x1, blocking collectives, local(): gathered = lax.all_gather(payload, 'mp', axis=0, tiled=False)  8.41 us
    all_to_all x1, starting transfers between devices, local(): recv = lax.all_to_all(send, 'dp', split_axis=0, concat_axis=0, tiled=True)  7.32 us
    ppermute x3, waiting for transfers between devices, local(): heads.append(lax.ppermute(combined, 'mp', route))  6.54 us
    pallas_call x1, Pallas kernels, local(): pl.pallas_call(functools.partial(start_kernel, maxb, per_pair, mp, step),...  4.23 us
    pallas_call x1, Pallas kernels, local(): pl.pallas_call(functools.partial(errors_kernel, mp - near), in_specs=[VME...  2.88 us
    pallas_call x1, Pallas kernels, local(): pl.pallas_call(functools.partial(early_kernel, near, features), in_specs=...  2.8 us
    pallas_call x1, Pallas kernels, local(): pl.pallas_call(functools.partial(owner_kernel, per_pair, near, mp, featur...  2.26 us
    ppermute x3, starting transfers between devices, local(): heads.append(lax.ppermute(combined, 'mp', route))  2.13 us
  transfers between devices with their start and end apart: 4, of which 2 were waited for; matrix products, arithmetic and copies ran while one was open for 0% of the time, Pallas kernels for 14%

profile of v1, /device:TPU:0, one launch (start us, length us, event | category | flops | bytes accessed | tf_op | source)
XLA Modules:
  0.0 39.2 jit_solution(7128896460786629290)
XLA Ops:
  0.6 4.2 %start.1 = (bf16[128,768]{1,0:T(8,128)(2,1)S(1)}, bf16[192,64]{1,0:T(8,128)(2,1)S(1)}, bf16[8,80,128]{2,1,0:T(8,128)(2,1)}, bf16[4,64,256]{2,1,0:T(8,128)(2,1)S(...) custom-call(s32[6]{0:T(128)} %frames_h.3, s32[30]{0:T(128)} %owners_h.1, s32[30]{0:T(128)} %offsets_h.1, ...), custom_call_target="tpu_custom_call" | custom-call | tf_op jit(solution)/shard_map/start/pallas_call | solution.py:440
  4.9 7.3 %all-to-all-start = ((bf16[8,80,128]{2,1,0:T(8,128)(2,1)}), bf16[8,80,128]{2,1,0:T(8,128)(2,1)S(1)}, u32[]{:S(2)}, u32[]{:S(2)}) async-start(bf16[8,80,128]{2,1,0:T(8,128)(2,1)} %get-tuple-element.14), calls=%async_computation | async-start | bytes 327680 | tf_op jit(solution)/shard_map/all_to_all | solution.py:500
  12.2 0.0 collective-permute-start
  12.2 1.6 %collective-permute-start.2 = (bf16[128,768]{1,0:T(8,128)(2,1)S(1)}, bf16[128,768]{1,0:T(8,128)(2,1)S(1)}, u32[]{:S(2)}, u32[]{:S(2)}) collective-permute-start(bf16[128,768]{1,0:T(8,128)(2,1)S(1)} %get-tuple-element.19.refs_0_), channel_id=1, source_target_pairs={{0,3},{1,2},{2,1},{3,0},{4,7},{5,6},{6,5},{7,4},{8,11},{9,10},{10,... | collective-permute-start | bytes 589832 | tf_op jit(solution)/shard_map/ppermute | solution.py:499
  13.8 0.5 %collective-permute-start.1 = (bf16[128,768]{1,0:T(8,128)(2,1)S(1)}, bf16[128,768]{1,0:T(8,128)(2,1)S(1)}, u32[]{:S(2)}, u32[]{:S(2)}) collective-permute-start(bf16[128,768]{1,0:T(8,128)(2,1)S(1)} %get-tuple-element.19.refs_0_), channel_id=1, source_target_pairs={{0,2},{1,3},{2,0},{3,1},{4,6},{5,7},{6,4},{7,5},{8,10},{9,11},{10,... | collective-permute-start | bytes 589832 | tf_op jit(solution)/shard_map/ppermute | solution.py:499
  14.3 0.0 collective-permute-done.refs_1_
  14.3 2.8 %early.1 = (f32[4,64,256]{2,1,0:T(8,128)S(1)}, f32[4,1,256]{2,1,0:T(1,128)S(1)}, bf16[1536,64]{1,0:T(8,128)(2,1)S(1)}) custom-call(s32[1,128]{1,0:T(1,128)S(1)} %get-tuple-element.15.picks, bf16[4,64,256]{2,1,0:T(8,128)(2,1)S(1)} %get-tuple-element.16.block_x, bf16[192,64]{1,0:T(8,128)(2,1)S(1)} %get-tuple-element.18.gram, ...), custom_call_target="tpu_custom_call" | custom-call | tf_op jit(solution)/shard_map/early/pallas_call | solution.py:502
  17.1 1.9 %collective-permute-done.2.refs_1_.refs_3_ = bf16[128,768]{1,0:T(8,128)(2,1)S(1)} collective-permute-done((bf16[128,768]{1,0:T(8,128)(2,1)S(1)}, bf16[128,768]{1,0:T(8,128)(2,1)S(1)}, u32[]{:S(2)}, u32[]{:S(2)}) %collective-permute-start.2) | collective-permute-done | bytes 196640 | tf_op jit(solution)/shard_map/ppermute | solution.py:499
  19.1 4.6 %collective-permute-done.1.refs_0_.refs_2_ = bf16[128,768]{1,0:T(8,128)(2,1)S(1)} collective-permute-done((bf16[128,768]{1,0:T(8,128)(2,1)S(1)}, bf16[128,768]{1,0:T(8,128)(2,1)S(1)}, u32[]{:S(2)}, u32[]{:S(2)}) %collective-permute-start.1) | collective-permute-done | bytes 196640 | tf_op jit(solution)/shard_map/ppermute | solution.py:499
  23.7 2.9 %errors.1 = (f32[1,128]{1,0:T(1,128)S(1)}, bf16[1536,64]{1,0:T(8,128)(2,1)S(1)}) custom-call(s32[1,128]{1,0:T(1,128)S(1)} %get-tuple-element.15.picks, bf16[4,64,256]{2,1,0:T(8,128)(2,1)S(1)} %get-tuple-element.16.block_x, bf16[4,64,256]{2,1,0:T(8,128)(2,1)S(1)} %get-tuple-element.17.block_n, f32[4,64,256]{2,1,0:T(8,128)S(1)} %get-tuple-element.20.partial, ...), custom_call_target="tpu_custom_call" | custom-call | tf_op jit(solution)/shard_map/errors/pallas_call | solution.py:517
  26.6 0.0 all-to-all-done.recv
  26.6 2.3 %owner.1 = bf16[544,128]{1,0:T(8,128)(2,1)S(1)} custom-call(bf16[8,80,128]{2,1,0:T(8,128)(2,1)S(1)} %all-to-all-done.recv, f32[1,128]{1,0:T(1,128)S(1)} %get-tuple-element.22.errs, bf16[192,64]{1,0:T(8,128)(2,1)S(1)} %get-tuple-element.18.gram, bf16[1536,64]{1,0:T(8,128)(2,1)S(1)} %get-tuple-element.23.mt_near, ...), custom_call_target="tpu_custom_call" | custom-call | tf_op jit(solution)/shard_map/owner/pallas_call | solution.py:535
  28.8 8.4 %all-gather = bf16[2176,128]{1,0:T(8,128)(2,1)S(1)} all-gather(bf16[544,128]{1,0:T(8,128)(2,1)S(1)} %owner.1), channel_id=2, replica_groups=mesh['dp'=8,'mp'=4] {'mp'}, dimensions={0}, use_global_device_ids=true | all-gather | bytes 696320 | tf_op jit(solution)/shard_map/all_gather | solution.py:545
  37.3 1.9 %place.1 = (bf16[18,64,128]{2,1,0:T(8,128)(2,1)}, f32[6]{0:T(128)}, f32[6]{0:T(128)}) custom-call(s32[6]{0:T(128)} %frames_h.3, s32[6]{0:T(128)} %groups_h.3, f32[6]{0:T(128)} %rewards_h.3, bf16[8,80,128]{2,1,0:T(8,128)(2,1)S(1)} %all-to-all-done.recv, bf16[4,544,128]{2,1,0:T(8,128)(2,1)S(1)} %bitcast.3), custom_call_target="tpu_custom_call" | custom-call | tf_op jit(solution)/shard_map/place/pallas_call | solution.py:547
Async XLA Ops:
  4.9 21.7 %all-to-all-start = ((bf16[8,80,128]{2,1,0:T(8,128)(2,1)}), bf16[8,80,128]{2,1,0:T(8,128)(2,1)S(1)}, u32[]{:S(2)}, u32[]{:S(2)}) async-start(bf16[8,80,128]{2,1,0:T(8,128)(2,1)} %get-tuple-element.14), calls=%async_computation | async-start | bytes 327680 | tf_op jit(solution)/shard_map/all_to_all | solution.py:500
  12.2 2.1 %collective-permute-start = (bf16[128,768]{1,0:T(8,128)(2,1)S(1)}, bf16[128,768]{1,0:T(8,128)(2,1)S(1)}, u32[]{:S(2)}, u32[]{:S(2)}) collective-permute-start(bf16[128,768]{1,0:T(8,128)(2,1)S(1)} %get-tuple-element.19.refs_0_), channel_id=1, source_target_pairs={{0,1},{1,0},{2,3},{3,2},{4,5},{5,4},{6,7},{7,6},{8,9},{9,8},{10,11... | collective-permute-start | bytes 589832 | tf_op jit(solution)/shard_map/ppermute | solution.py:499
  12.2 6.9 %collective-permute-start.2 = (bf16[128,768]{1,0:T(8,128)(2,1)S(1)}, bf16[128,768]{1,0:T(8,128)(2,1)S(1)}, u32[]{:S(2)}, u32[]{:S(2)}) collective-permute-start(bf16[128,768]{1,0:T(8,128)(2,1)S(1)} %get-tuple-element.19.refs_0_), channel_id=1, source_target_pairs={{0,3},{1,2},{2,1},{3,0},{4,7},{5,6},{6,5},{7,4},{8,11},{9,10},{10,... | collective-permute-start | bytes 589832 | tf_op jit(solution)/shard_map/ppermute | solution.py:499
  13.8 9.9 %collective-permute-start.1 = (bf16[128,768]{1,0:T(8,128)(2,1)S(1)}, bf16[128,768]{1,0:T(8,128)(2,1)S(1)}, u32[]{:S(2)}, u32[]{:S(2)}) collective-permute-start(bf16[128,768]{1,0:T(8,128)(2,1)S(1)} %get-tuple-element.19.refs_0_), channel_id=1, source_target_pairs={{0,2},{1,3},{2,0},{3,1},{4,6},{5,7},{6,4},{7,5},{8,10},{9,11},{10,... | collective-permute-start | bytes 589832 | tf_op jit(solution)/shard_map/ppermute | solution.py:499

commit v2 on v1

--- a/solution.py
+++ b/solution.py
@@ -8,7 +8,7 @@
 from jax.sharding import PartitionSpec as P
 
 GSIZE = 12
-META = 16
+META = 8
 LANES = 128
 F32 = jnp.float32
 BF16 = jnp.bfloat16
@@ -72,6 +72,7 @@
     block_x,
     block_n,
     picks,
+    info,
     frames,
     owners,
     offsets,
@@ -80,6 +81,7 @@
     embed,
     gain,
     held,
+    packed,
     places,
     rows,
     source,
@@ -91,6 +93,7 @@
     row_sems,
     x_sems,
     n_sems,
+    leave_sem,
 ):
     peers = send.shape[0]
     _, channels, width = latent.shape
@@ -158,7 +161,7 @@
     copies = [
         pltpu.make_async_copy(
             latent.at[source[o * per_pair + q]],
-            send.at[o, pl.ds(q * channels, channels)],
+            packed.at[o, pl.ds(q * channels, channels)],
             row_sems.at[o * per_pair + q],
         )
         for o in range(peers)
@@ -170,23 +173,27 @@
         copies.append(pltpu.make_async_copy(noise.at[slot_of[j]], block_n.at[j // 2, :, lanes], n_sems.at[j]))
     for copy in copies:
         copy.start()
-
-    lane = lax.broadcasted_iota(jnp.int32, (1, LANES), 1)
-    found = jnp.where(lane == LANES - 1, count, 0)
+    leave = pltpu.make_async_copy(packed, send, leave_sem)
+
+    sub = lax.broadcasted_iota(jnp.int32, picks.shape, 0)
+    found = jnp.full(picks.shape, -1, jnp.int32)
     for j in range(share):
-        found = jnp.where(lane == j, chosen[j], found)
+        found = jnp.where((sub == j) & (j < count), chosen[j], found)
     picks[...] = found
 
-    hi, mid, lo = split3(lane_row(lambda s: rewards[s], samples, F32))
+    reward = lane_row(lambda s: rewards[s], samples, F32)
     group = lane_row(lambda s: groups[s].astype(F32), samples, F32)
+    counts = lane_row(lambda s: live_count(frames, s).astype(F32), samples, F32)
+    hi, mid, lo = split3(reward)
     sub = lax.broadcasted_iota(jnp.int32, (META, LANES), 0)
+    info[...] = jnp.where(sub == 0, reward, jnp.where(sub == 1, group, counts))
     shared = jnp.where(sub == 1, hi.astype(F32), 0.0)
     shared = jnp.where(sub == 2, mid.astype(F32), shared)
     shared = jnp.where(sub == 3, lo.astype(F32), shared)
     shared = jnp.where(sub == 4, group, shared)
     for o in range(peers):
         first = lane_row(lambda q: rows[o * per_pair + q].astype(F32), per_pair, F32)
-        send[o, pl.ds(per_pair * channels, META), :] = jnp.where(sub == 0, first, shared).astype(BF16)
+        packed[o, pl.ds(per_pair * channels, META), :] = jnp.where(sub == 0, first, shared).astype(BF16)
 
     big[0].wait()
     e = embed[...]
@@ -199,30 +206,47 @@
         copy.wait()
         m = jnp.dot(both, held[:, n * step : (n + 1) * step], preferred_element_type=F32)
         out[:channels, n * step : (n + 1) * step] = (m[:channels] + m[channels:]).astype(BF16)
+        if n == 0:
+            for one in copies[:total]:
+                one.wait()
+            leave.start()
     hi, mid, lo = split3(lax.dot_general(e, e, (((1,), (1,)), ((), ())), preferred_element_type=F32))
     gram[...] = jnp.concatenate([hi, mid, lo], axis=0)
     big[2].wait()
-    for copy in copies:
+    for copy in copies[total:]:
         copy.wait()
-
-
-def norm_factor(x, gram, features):
-    channels = x.shape[0]
+    leave.wait()
+
+
+def norm_factors(xs, gram, features):
+    channels, width = xs[0].shape
+    x = jnp.concatenate(xs, axis=1)
     g = jnp.dot(gram, x, preferred_element_type=F32)
     gx = g[:channels] + g[channels : 2 * channels] + g[2 * channels :]
     mean_sq = jnp.sum(gx * x.astype(F32), axis=0, keepdims=True) * (1.0 / features)
-    return 0.5 * lax.rsqrt(jnp.maximum(mean_sq, 0.0) + 0.25)
-
-
-def velocity(x, half, mt, heads, total=None):
-    channels, hidden = heads[0].shape[0] // 2, heads[0].shape[1]
-    for m, head in enumerate(heads):
-        mid = jnp.dot(mt[m * hidden : (m + 1) * hidden, :], x, preferred_element_type=F32)
-        v = mid * half
-        act = (v + v * jnp.tanh(v)).astype(BF16)
-        part = jnp.dot(head[channels:, :], act, preferred_element_type=F32)
-        total = part if total is None else total + part
-    return total
+    half = 0.5 * lax.rsqrt(jnp.maximum(mean_sq, 0.0) + 0.25)
+    return [half[:, p * width : (p + 1) * width] for p in range(len(xs))]
+
+
+def velocities(xs, halves, parts, totals):
+    totals = list(totals)
+    waiting = []
+
+    def finish():
+        p, head, act = waiting.pop()
+        part = jnp.dot(head, act, preferred_element_type=F32)
+        totals[p] = part if totals[p] is None else totals[p] + part
+
+    for p, x in enumerate(xs):
+        for mt, both, row in parts:
+            channels, hidden = both.shape[0] // 2, both.shape[1]
+            mid = jnp.dot(mt[row : row + hidden, :], x, preferred_element_type=F32)
+            if waiting:
+                finish()
+            v = mid * halves[p]
+            waiting.append((p, both[channels:, :], (v + v * jnp.tanh(v)).astype(BF16)))
+    finish()
+    return totals
 
 
 def turn(mt, heads):
@@ -231,51 +255,39 @@
         mt[m * hidden : (m + 1) * hidden, :] = head[:channels, :].T
 
 
-def early_kernel(near, features, picks, block_x, gram, *refs):
-    heads, (partial, halves, mt, table, sem) = refs[:near], refs[near:]
-    copy = pltpu.make_async_copy(picks, table, sem)
-    copy.start()
+def shards_of(mt, heads):
+    hidden = heads[0].shape[1]
+    return [(mt, head, m * hidden) for m, head in enumerate(heads)]
+
+
+def early_kernel(near, features, block_x, gram, *refs):
+    heads, (partial, halves, mt) = refs[:near], refs[near:]
     turn(mt, heads)
-    copy.wait()
-    count = table[0, LANES - 1]
-
-    def body(pair, carry):
-        x = block_x[pair]
-        half = norm_factor(x, gram[...], features)
-        halves[pair] = half
-        partial[pair] = velocity(x, half, mt, heads)
-        return carry
-
-    lax.fori_loop(0, (count + 1) // 2, body, 0)
+    xs = [block_x[p] for p in range(block_x.shape[0])]
+    half = norm_factors(xs, gram[...], features)
+    for p, total in enumerate(velocities(xs, half, shards_of(mt, heads), [None] * len(xs))):
+        halves[p] = half[p]
+        partial[p] = total
 
 
 def errors_kernel(far, picks, block_x, block_n, partial, halves, *refs):
-    heads, (errs, mt, acc, table, sem) = refs[:far], refs[far:]
-    width = block_x.shape[2] // 2
-    copy = pltpu.make_async_copy(picks, table, sem)
-    copy.start()
+    heads, (errs, mt) = refs[:far], refs[far:]
+    pairs, _, double = block_x.shape
+    width = double // 2
     turn(mt, heads)
-    acc[...] = jnp.zeros_like(acc)
-    copy.wait()
-    count = table[0, LANES - 1]
-
-    def body(pair, carry):
-        v = velocity(block_x[pair], halves[pair], mt, heads, partial[pair])
-        e = block_n[pair].astype(F32) + v
-        rows = jnp.sum(e * e, axis=0, keepdims=True)
-        acc[pl.ds(table[0, 2 * pair], 1), :] += rows[:, :width]
-
-        @pl.when(2 * pair + 1 < count)
-        def _():
-            acc[pl.ds(table[0, 2 * pair + 1], 1), :] += rows[:, width:]
-
-        return carry
-
-    lax.fori_loop(0, (count + 1) // 2, body, 0)
-    sums = jnp.sum(acc[...], axis=1, keepdims=True)
-    lane = lax.broadcasted_iota(jnp.int32, acc.shape, 1)
-    sub = lax.broadcasted_iota(jnp.int32, acc.shape, 0)
-    errs[...] = jnp.sum(jnp.where(lane == sub, sums, 0.0), axis=0, keepdims=True)
+    xs = [block_x[p] for p in range(pairs)]
+    half = [halves[p] for p in range(pairs)]
+    totals = velocities(xs, half, shards_of(mt, heads), [partial[p] for p in range(pairs)])
+    sub = lax.broadcasted_iota(jnp.int32, picks.shape, 0)
+    lane = lax.broadcasted_iota(jnp.int32, picks.shape, 1)
+    sums = jnp.zeros(picks.shape, F32)
+    for p, v in enumerate(totals):
+        e = block_n[p].astype(F32) + v
+        line = jnp.sum(e * e, axis=0, keepdims=True)
+        sums = jnp.where(sub == 2 * p, line[:, :width], sums)
+        sums = jnp.where(sub == 2 * p + 1, line[:, width:], sums)
+    each = jnp.sum(sums, axis=1, keepdims=True)
+    errs[...] = jnp.sum(jnp.where(lane == picks[...], each, 0.0), axis=0, keepdims=True)
 
 
 def owner_kernel(per_pair, near, shards, features, recv, errs, gram, mt_near, mt_far, *refs):
@@ -302,63 +314,49 @@
         for n in range(low, min(low + 16, total)):
             order[count] = n
             count = count + lax.bitwise_and(lax.shift_right_logical(mask, n - low), 1)
-
-    def body(pair, carry):
-        one = order[2 * pair]
-        more = 2 * pair + 1 < count
-        two = jnp.where(more, order[2 * pair + 1], one)
-        x = jnp.concatenate(
-            [
-                recv[n // per_pair, pl.ds(pl.multiple_of((n % per_pair) * channels, channels), channels), :]
-                for n in (one, two)
-            ],
-            axis=1,
-        )
-        half = norm_factor(x, gram[...], features)
-        v = velocity(x, half, mt_near, heads[:near])
-        v = velocity(x, half, mt_far, heads[near:], v).astype(BF16)
-        width = v.shape[1] // 2
-        out[pl.ds(pl.multiple_of(one * channels, channels), channels), :] = v[:, :width]
-
-        @pl.when(more)
-        def _():
-            out[pl.ds(pl.multiple_of(two * channels, channels), channels), :] = v[:, width:]
+    parts = shards_of(mt_near, heads[:near]) + shards_of(mt_far, heads[near:])
+
+    def block_of(n):
+        if per_pair == 1:
+            return recv[n, :channels, :]
+        return recv[n // per_pair, pl.ds(pl.multiple_of((n % per_pair) * channels, channels), channels), :]
+
+    def run(begin, pairs):
+        slots = [order[jnp.minimum(begin + j, count - 1)] for j in range(2 * pairs)]
+        xs = [
+            jnp.concatenate([block_of(slots[2 * p]), block_of(slots[2 * p + 1])], axis=1)
+            for p in range(pairs)
+        ]
+        half = norm_factors(xs, gram[...], features)
+        for p, v in enumerate(velocities(xs, half, parts, [None] * pairs)):
+            v = v.astype(BF16)
+            width = v.shape[1] // 2
+            for j in range(2):
+                at = pl.multiple_of(slots[2 * p + j] * channels, channels)
+                out[pl.ds(at, channels), :] = v[:, j * width : (j + 1) * width]
+
+    def quad(n, carry):
+        left = (jnp.clip(count - 8 * n, 0, 8) + 1) // 2
+        for pairs in range(1, 5):
+
+            @pl.when(left == pairs)
+            def _():
+                run(8 * n, pairs)
 
         return carry
 
-    lax.fori_loop(0, (count + 1) // 2, body, 0)
-
-
-def place_kernel(
-    per_pair,
-    frames_h,
-    groups_h,
-    rewards_h,
-    recv,
-    gathered,
-    pred,
-    log_out,
-    adv_out,
-    frames,
-    groups,
-    rewards,
-    log_prob,
-    advantage,
-    small_sems,
-    sem,
-):
+    if total <= 8:
+        quad(0, 0)
+    else:
+        lax.fori_loop(0, (total + 7) // 8, quad, 0)
+
+
+def place_kernel(per_pair, samples, info, recv, gathered, pred, log_out, adv_out, log_prob, advantage, small_sems, sem):
     shards = gathered.shape[0]
     rows_here, channels, width = pred.shape
     peers = recv.shape[0]
     total = peers * per_pair
-    samples = frames.shape[0]
     base = total * channels
-    small = [
-        pltpu.make_async_copy(a, b, small_sems.at[n])
-        for n, (a, b) in enumerate([(frames_h, frames), (groups_h, groups), (rewards_h, rewards)])
-    ]
-    for copy in small:
-        copy.start()
     bits = rows_here.bit_length()
     pack = 24 // bits
     lane8 = lax.broadcasted_iota(jnp.int32, (peers, LANES), 1)
@@ -378,26 +376,30 @@
                         gathered.at[m, pl.ds(n * channels, channels)], pred.at[row - 1], sem
                     ).start()
 
-    for copy in small:
-        copy.wait()
     lane = lax.broadcasted_iota(jnp.int32, (1, LANES), 1)
     sums = jnp.zeros((1, LANES), F32)
     for m in range(shards):
         part = gathered[m, gathered.shape[1] - META :, :].astype(F32)
         sums = sums + (part[0:1] + part[1:2] + part[2:3])
-    size = lane_row(lambda s: (live_count(frames, s) * (channels * width)).astype(F32), samples, F32)
-    logs = -0.5 * sums / jnp.where(lane < samples, size, 1.0)
-
-    info = recv[:, pl.ds(per_pair * channels, META), :].astype(F32)
-    every = info[:, 1, :] + info[:, 2, :] + info[:, 3, :]
-    group = info[:, 4, :]
-    inside = lax.broadcasted_iota(jnp.int32, every.shape, 1) < samples
+    reward, own_group, counts = info[0:1, :], info[1:2, :], info[2:3, :]
+    size = jnp.where(lane < samples, counts * float(channels * width), 1.0)
+    logs = -0.5 * sums / size
+
+    meta = recv[:, pl.ds(per_pair * channels, META), :].astype(F32)
+    every = meta[:, 1, :] + meta[:, 2, :] + meta[:, 3, :]
+    group = jnp.where(lax.broadcasted_iota(jnp.int32, every.shape, 1) < samples, meta[:, 4, :], -1.0)
+    mean = jnp.zeros((1, LANES), F32)
+    meansq = jnp.zeros((1, LANES), F32)
     for s in range(samples):
-        chosen = inside & (group == groups[s].astype(F32))
-        mean = jnp.sum(jnp.where(chosen, every, 0.0), keepdims=True) / GSIZE
-        meansq = jnp.sum(jnp.where(chosen, every * every, 0.0), keepdims=True) / GSIZE
-        value = (rewards[s] - mean) / jnp.sqrt(meansq - mean * mean + 0.25)
-        advantage[s] = jnp.sum(value)
+        mine = jnp.sum(jnp.where(lane == s, own_group, 0.0), axis=1, keepdims=True)
+        chosen = group == mine
+        one = jnp.sum(jnp.sum(jnp.where(chosen, every, 0.0), axis=0, keepdims=True), axis=1, keepdims=True)
+        two = jnp.sum(jnp.sum(jnp.where(chosen, every * every, 0.0), axis=0, keepdims=True), axis=1, keepdims=True)
+        mean = jnp.where(lane == s, one / GSIZE, mean)
+        meansq = jnp.where(lane == s, two / GSIZE, meansq)
+    scores = (reward - mean) / jnp.sqrt(meansq - mean * mean + 0.25)
+    for s in range(samples):
+        advantage[s] = jnp.sum(jnp.where(lane == s, scores, 0.0))
         log_prob[s] = jnp.sum(jnp.where(lane == s, logs, 0.0))
     last = [
         pltpu.make_async_copy(log_prob, log_out, small_sems.at[0]),
@@ -437,17 +439,18 @@
     params = functools.partial(pltpu.CompilerParams, vmem_limit_bytes=48 * 1024 * 1024)
     step = next(n for n in (256, 128, hidden) if hidden % n == 0)
 
-    combined, gram, send, block_x, block_n, picks = pl.pallas_call(
+    combined, gram, send, block_x, block_n, picks, info = pl.pallas_call(
         functools.partial(start_kernel, maxb, per_pair, mp, step),
         in_specs=[HBM] * 11,
-        out_specs=[VMEM] * 6,
+        out_specs=[VMEM] * 2 + [ANY] + [VMEM] * 4,
         out_shape=[
             jax.ShapeDtypeStruct((2 * channels, hidden), BF16),
             jax.ShapeDtypeStruct((3 * channels, channels), BF16),
-            pltpu.VMEM((peers, per_pair * channels + META, width), BF16),
+            jax.ShapeDtypeStruct((peers, per_pair * channels + META, width), BF16),
             jax.ShapeDtypeStruct((share, channels, 2 * width), BF16),
             jax.ShapeDtypeStruct((share, channels, 2 * width), BF16),
-            jax.ShapeDtypeStruct((1, LANES), jnp.int32),
+            jax.ShapeDtypeStruct((2 * share, LANES), jnp.int32),
+            jax.ShapeDtypeStruct((META, LANES), F32),
         ],
         scratch_shapes=[
             pltpu.SMEM((samples,), jnp.int32),
@@ -458,6 +461,7 @@
             pltpu.VMEM((channels, features), BF16),
             pltpu.VMEM((1, features), F32),
             pltpu.VMEM((features, hidden), BF16),
+            pltpu.VMEM((peers, per_pair * channels + META, width), BF16),
             pltpu.SMEM((peers + 1,), jnp.int32),
             pltpu.SMEM((total + 1,), jnp.int32),
             pltpu.SMEM((total + 1,), jnp.int32),
@@ -469,6 +473,7 @@
             pltpu.SemaphoreType.DMA((total,)),
             pltpu.SemaphoreType.DMA((2 * share,)),
             pltpu.SemaphoreType.DMA((2 * share,)),
+            pltpu.SemaphoreType.DMA,
         ],
         compiler_params=params(),
         name="start",
@@ -491,29 +496,31 @@
         )
     )
 
-    paired = mp & (mp - 1) == 0
+    heads = [combined]
+    near = mp
+    while near > 1:
+        near //= 2
+        route = [(j, j ^ near) for j in range(mp)]
+        more = []
+        for head in heads:
+            more.append(lax.ppermute(head, "mp", route))
+        heads += more
     near = max(mp // 2, 1)
-    heads = [combined]
-    for s in range(1, mp):
-        route = [(j, j ^ s if paired else (j + s) % mp) for j in range(mp)]
-        heads.append(lax.ppermute(combined, "mp", route))
     recv = lax.all_to_all(send, "dp", split_axis=0, concat_axis=0, tiled=True)
 
     partial, halves, mt_near = pl.pallas_call(
         functools.partial(early_kernel, near, features),
-        in_specs=[VMEM] * (3 + near),
+        in_specs=[VMEM] * (2 + near),
         out_specs=[VMEM] * 3,
         out_shape=[
             jax.ShapeDtypeStruct((share, channels, 2 * width), F32),
             jax.ShapeDtypeStruct((share, 1, 2 * width), F32),
             jax.ShapeDtypeStruct((near * hidden, channels), BF16),
         ],
-        scratch_shapes=[pltpu.SMEM((1, LANES), jnp.int32), pltpu.SemaphoreType.DMA],
         compiler_params=params(),
         name="early",
-    )(picks, block_x, gram, *heads[:near])
-
-    rows8 = (samples + 7) // 8 * 8
+    )(block_x, gram, *heads[:near])
+
     errs, mt_far = pl.pallas_call(
         functools.partial(errors_kernel, mp - near),
         in_specs=[VMEM] * (5 + mp - near),
@@ -521,11 +528,6 @@
         out_shape=[
             jax.ShapeDtypeStruct((1, LANES), F32),
             jax.ShapeDtypeStruct(((mp - near) * hidden, channels), BF16),
-        ],
-        scratch_shapes=[
-            pltpu.VMEM((rows8, width), F32),
-            pltpu.SMEM((1, LANES), jnp.int32),
-            pltpu.SemaphoreType.DMA,
         ],
         compiler_params=params(),
         name="errors",
@@ -545,8 +547,8 @@
     gathered = lax.all_gather(payload, "mp", axis=0, tiled=False)
 
     return pl.pallas_call(
-        functools.partial(place_kernel, per_pair),
-        in_specs=[HBM] * 3 + [VMEM, VMEM],
+        functools.partial(place_kernel, per_pair, samples),
+        in_specs=[VMEM] * 3,
         out_specs=[ANY] * 3,
         out_shape=[
             jax.ShapeDtypeStruct((owner_rows, channels, width), BF16),
@@ -554,17 +556,14 @@
             jax.ShapeDtypeStruct((samples,), F32),
         ],
         scratch_shapes=[
-            pltpu.SMEM((samples,), jnp.int32),
-            pltpu.SMEM((samples,), jnp.int32),
             pltpu.SMEM((samples,), F32),
             pltpu.SMEM((samples,), F32),
-            pltpu.SMEM((samples,), F32),
-            pltpu.SemaphoreType.DMA((3,)),
+            pltpu.SemaphoreType.DMA((2,)),
             pltpu.SemaphoreType.DMA,
         ],
         compiler_params=params(),
         name="place",
-    )(in_hbm(frames), in_hbm(groups), in_hbm(rewards), recv, gathered)
+    )(info, recv, gathered)
 
 
 def solution(mesh):
@@ -581,6 +580,10 @@
         P(None, "mp"),
         P("mp", None),
     )
+    mp = mesh.shape["mp"]
+    near = mp
+    while near > 1:
+        near //= 2
     return jax.shard_map(
         local,
         mesh=mesh,

time: 39.5 us -> 31.8 us (0.81)
  waiting for transfers between devices: 6.54 us -> 3.13 us
  Pallas kernels: 14.1 us -> 11 us
  blocking collectives: 8.41 us -> 7.17 us
    ppermute x3, waiting for transfers between devices: 6.54 us -> 0.01 us  [local(): more.append(lax.ppermute(head, 'mp', route))]
    all_to_all x1, waiting for transfers between devices: 0.01 us -> 3.13 us  [local(): recv = lax.all_to_all(send, 'dp', split_axis=0, concat_axis=0, tiled=True)]
    all_to_all x1, starting transfers between devices: 7.32 us -> 5.83 us  [local(): recv = lax.all_to_all(send, 'dp', split_axis=0, concat_axis=0, tiled=True)]
    ppermute x3, starting transfers between devices: 2.13 us -> 3.53 us  [local(): more.append(lax.ppermute(head, 'mp', route))]
    all_gather x1, blocking collectives: 8.41 us -> 7.17 us  [local(): gathered = lax.all_gather(payload, 'mp', axis=0, tiled=False)]
    pallas_call x1, Pallas kernels: 2.88 us -> 1.79 us  [local(): pl.pallas_call(functools.partial(errors_kernel, mp - near), in_specs=[VME...]
    pallas_call x1, Pallas kernels: 1.9 us -> 0.97 us  [local(): pl.pallas_call(functools.partial(place_kernel, per_pair, samples), in_spe...]
    pallas_call x1, Pallas kernels: 2.8 us -> 1.99 us  [local(): pl.pallas_call(functools.partial(early_kernel, near, features), in_specs=...]
  transfers between devices with their start and end apart: 4 -> 4, of which waited for: 2 -> 1; matrix products, arithmetic and copies ran while one was open for 0% -> 0% of each run, Pallas kernels for 14% -> 12%
where the time goes in v2:
time: 31.8 us; the launch traced here: 31.6 us
  Pallas kernels  11 us (35%)
  starting transfers between devices  9.36 us (29%)
  blocking collectives  7.17 us (23%)
  waiting for transfers between devices  3.13 us (10%)
  between operations  0.85 us (3%)
    all_gather x1, blocking collectives, local(): gathered = lax.all_gather(payload, 'mp', axis=0, tiled=False)  7.17 us
    all_to_all x1, starting transfers between devices, local(): recv = lax.all_to_all(send, 'dp', split_axis=0, concat_axis=0, tiled=True)  5.83 us
    pallas_call x1, Pallas kernels, local(): pl.pallas_call(functools.partial(start_kernel, maxb, per_pair, mp, step),...  4.15 us
    ppermute x3, starting transfers between devices, local(): more.append(lax.ppermute(head, 'mp', route))  3.53 us
    all_to_all x1, waiting for transfers between devices, local(): recv = lax.all_to_all(send, 'dp', split_axis=0, concat_axis=0, tiled=True)  3.13 us
    pallas_call x1, Pallas kernels, local(): pl.pallas_call(functools.partial(owner_kernel, per_pair, near, mp, featur...  2.13 us
    pallas_call x1, Pallas kernels, local(): pl.pallas_call(functools.partial(early_kernel, near, features), in_specs=...  1.99 us
    pallas_call x1, Pallas kernels, local(): pl.pallas_call(functools.partial(errors_kernel, mp - near), in_specs=[VME...  1.79 us
  transfers between devices with their start and end apart: 4, of which 1 were waited for; matrix products, arithmetic and copies ran while one was open for 0% of the time, Pallas kernels for 12%

profile of v2, /device:TPU:0, one launch (start us, length us, event | category | flops | bytes accessed | tf_op | source)
XLA Modules:
  0.0 31.6 jit_solution(1148827356236838921)
XLA Ops:
  0.6 4.2 %start.1 = (bf16[128,768]{1,0:T(8,128)(2,1)S(1)}, bf16[192,64]{1,0:T(8,128)(2,1)S(1)}, bf16[8,72,128]{2,1,0:T(8,128)(2,1)}, bf16[4,64,256]{2,1,0:T(8,128)(2,1)S(...) custom-call(s32[6]{0:T(128)} %frames_h.1, s32[30]{0:T(128)} %owners_h.1, ...), custom_call_target="tpu_custom_call" | custom-call | tf_op jit(solution)/shard_map/start/pallas_call | solution.py:442
  4.8 3.0 %collective-permute-start = (bf16[128,768]{1,0:T(8,128)(2,1)S(1)}, bf16[128,768]{1,0:T(8,128)(2,1)S(1)}, u32[]{:S(2)}, u32[]{:S(2)}) collective-permute-start(bf16[128,768]{1,0:T(8,128)(2,1)S(1)} %get-tuple-element.21.refs_0_), channel_id=1, source_target_pairs={{0,2},{1,3},{2,0},{3,1},{4,6},{5,7},{6,4},{7,5},{8,10},{9,11},{10,... | collective-permute-start | bytes 589832 | tf_op jit(solution)/shard_map/ppermute | solution.py:506
  7.8 5.8 %all-to-all-start = ((bf16[8,72,128]{2,1,0:T(8,128)(2,1)}), bf16[8,72,128]{2,1,0:T(8,128)(2,1)S(1)}, u32[]{:S(2)}, u32[]{:S(2)}) async-start(bf16[8,72,128]{2,1,0:T(8,128)(2,1)} %get-tuple-element.16), calls=%async_computation | async-start | bytes 294912 | tf_op jit(solution)/shard_map/all_to_all | solution.py:509
  13.7 0.0 collective-permute-start.1
  13.7 0.0 collective-permute-done.refs_1_
  13.7 0.5 %collective-permute-start.2 = (bf16[128,768]{1,0:T(8,128)(2,1)S(1)}, bf16[128,768]{1,0:T(8,128)(2,1)S(1)}, u32[]{:S(2)}, u32[]{:S(2)}) collective-permute-start(bf16[128,768]{1,0:T(8,128)(2,1)S(1)} %collective-permute-done.refs_1_), channel_id=1, source_target_pairs={{0,1},{1,0},{2,3},{3,2},{4,5},{5,4},{6,7},{7,6},{8,9},{9,8},{10,11... | collective-permute-start | bytes 589832 | tf_op jit(solution)/shard_map/ppermute | solution.py:506
  14.2 2.0 %early.1 = (f32[4,64,256]{2,1,0:T(8,128)S(1)}, f32[4,1,256]{2,1,0:T(1,128)S(1)}, bf16[1536,64]{1,0:T(8,128)(2,1)S(1)}) custom-call(bf16[4,64,256]{2,1,0:T(8,128)(2,1)S(1)} %get-tuple-element.18.block_x, bf16[192,64]{1,0:T(8,128)(2,1)S(1)} %get-tuple-element.20.gram, bf16[128,768]{1,0:T(8,128)(2,1)S(1)} %get-tuple-element.21.refs_0_, ...), custom_call_target="tpu_custom_call" | custom-call | tf_op jit(solution)/shard_map/early/pallas_call | solution.py:511
  16.2 0.0 collective-permute-done.1.refs_0_.refs_2_
  16.2 0.0 collective-permute-done.2.refs_1_.refs_3_
  16.2 1.8 %errors.1 = (f32[1,128]{1,0:T(1,128)S(1)}, bf16[1536,64]{1,0:T(8,128)(2,1)S(1)}) custom-call(s32[8,128]{1,0:T(8,128)S(1)} %get-tuple-element.17.picks, bf16[4,64,256]{2,1,0:T(8,128)(2,1)S(1)} %get-tuple-element.18.block_x, bf16[4,64,256]{2,1,0:T(8,128)(2,1)S(1)} %get-tuple-element.19.block_n, f32[4,64,256]{2,1,0:T(8,128)S(1)} %get-tuple-element.22.partial, ...), custom_call_target="tpu_custom_call" | custom-call | tf_op jit(solution)/shard_map/errors/pallas_call | solution.py:524
  18.0 3.1 %all-to-all-done.recv = bf16[8,72,128]{2,1,0:T(8,128)(2,1)S(1)} async-done(((bf16[8,72,128]{2,1,0:T(8,128)(2,1)}), bf16[8,72,128]{2,1,0:T(8,128)(2,1)S(1)}, u32[]{:S(2)}, u32[]{:S(2)}) %all-to-all-start) | async-done | bytes 147488 | tf_op jit(solution)/shard_map/all_to_all | solution.py:509
  21.1 2.1 %owner.1 = bf16[528,128]{1,0:T(8,128)(2,1)S(1)} custom-call(bf16[8,72,128]{2,1,0:T(8,128)(2,1)S(1)} %all-to-all-done.recv, f32[1,128]{1,0:T(1,128)S(1)} %get-tuple-element.24.errs, bf16[192,64]{1,0:T(8,128)(2,1)S(1)} %get-tuple-element.20.gram, bf16[1536,64]{1,0:T(8,128)(2,1)S(1)} %get-tuple-element.25.mt_near, ...), custom_call_target="tpu_custom_call" | custom-call | tf_op jit(solution)/shard_map/owner/pallas_call | solution.py:537
  23.3 7.2 %all-gather = bf16[2112,128]{1,0:T(8,128)(2,1)S(1)} all-gather(bf16[528,128]{1,0:T(8,128)(2,1)S(1)} %owner.1), channel_id=2, replica_groups=mesh['dp'=8,'mp'=4] {'mp'}, dimensions={0}, use_global_device_ids=true | all-gather | bytes 675840 | tf_op jit(solution)/shard_map/all_gather | solution.py:547
  30.4 1.0 %place.1 = (bf16[18,64,128]{2,1,0:T(8,128)(2,1)}, f32[6]{0:T(128)}, f32[6]{0:T(128)}) custom-call(f32[8,128]{1,0:T(8,128)S(1)} %get-tuple-element.15.info, bf16[8,72,128]{2,1,0:T(8,128)(2,1)S(1)} %all-to-all-done.recv, bf16[4,528,128]{2,1,0:T(8,128)(2,1)S(1)} %bitcast.3), custom_call_target="tpu_custom_call" | custom-call | tf_op jit(solution)/shard_map/place/pallas_call | solution.py:549
Async XLA Ops:
  4.8 8.9 %collective-permute-start = (bf16[128,768]{1,0:T(8,128)(2,1)S(1)}, bf16[128,768]{1,0:T(8,128)(2,1)S(1)}, u32[]{:S(2)}, u32[]{:S(2)}) collective-permute-start(bf16[128,768]{1,0:T(8,128)(2,1)S(1)} %get-tuple-element.21.refs_0_), channel_id=1, source_target_pairs={{0,2},{1,3},{2,0},{3,1},{4,6},{5,7},{6,4},{7,5},{8,10},{9,11},{10,... | collective-permute-start | bytes 589832 | tf_op jit(solution)/shard_map/ppermute | solution.py:506
  7.8 13.3 %all-to-all-start = ((bf16[8,72,128]{2,1,0:T(8,128)(2,1)}), bf16[8,72,128]{2,1,0:T(8,128)(2,1)S(1)}, u32[]{:S(2)}, u32[]{:S(2)}) async-start(bf16[8,72,128]{2,1,0:T(8,128)(2,1)} %get-tuple-element.16), calls=%async_computation | async-start | bytes 294912 | tf_op jit(solution)/shard_map/all_to_all | solution.py:509
  13.7 2.5 %collective-permute-start.1 = (bf16[128,768]{1,0:T(8,128)(2,1)S(1)}, bf16[128,768]{1,0:T(8,128)(2,1)S(1)}, u32[]{:S(2)}, u32[]{:S(2)}) collective-permute-start(bf16[128,768]{1,0:T(8,128)(2,1)S(1)} %get-tuple-element.21.refs_0_), channel_id=1, source_target_pairs={{0,1},{1,0},{2,3},{3,2},{4,5},{5,4},{6,7},{7,6},{8,9},{9,8},{10,11... | collective-permute-start | bytes 589832 | tf_op jit(solution)/shard_map/ppermute | solution.py:506
  13.7 2.5 %collective-permute-start.2 = (bf16[128,768]{1,0:T(8,128)(2,1)S(1)}, bf16[128,768]{1,0:T(8,128)(2,1)S(1)}, u32[]{:S(2)}, u32[]{:S(2)}) collective-permute-start(bf16[128,768]{1,0:T(8,128)(2,1)S(1)} %collective-permute-done.refs_1_), channel_id=1, source_target_pairs={{0,1},{1,0},{2,3},{3,2},{4,5},{5,4},{6,7},{7,6},{8,9},{9,8},{10,11... | collective-permute-start | bytes 589832 | tf_op jit(solution)/shard_map/ppermute | solution.py:506

commit v3 on v2

--- a/solution.py
+++ b/solution.py
@@ -50,54 +50,12 @@
     return lax.shift_right_logical(value, mp.bit_length() - 1) if mp & (mp - 1) == 0 else value // mp
 
 
-def start_kernel(
-    maxb,
-    per_pair,
-    mp,
-    step,
-    frames_h,
-    owners_h,
-    offsets_h,
-    groups_h,
-    rewards_h,
-    latent,
-    noise,
-    embed_h,
-    gain_h,
-    weight,
-    head_h,
-    out,
-    gram,
-    send,
-    block_x,
-    block_n,
-    picks,
-    info,
-    frames,
-    owners,
-    offsets,
-    groups,
-    rewards,
-    embed,
-    gain,
-    held,
-    packed,
-    places,
-    rows,
-    source,
-    chosen,
-    slot_of,
-    small_sems,
-    big_sems,
-    weight_sems,
-    row_sems,
-    x_sems,
-    n_sems,
-    leave_sem,
-):
-    peers = send.shape[0]
+def start_kernel(maxb, per_pair, peers, mp, step, *refs):
+    (frames_h, owners_h, offsets_h, groups_h, rewards_h, latent, noise, embed_h, gain_h, weight, head_h) = refs[:11]
+    (send, out, embed, block_x, block_n, picks, info) = refs[11:18]
+    (frames, owners, offsets, groups, rewards, gain, held, blocks, meta, places, rows, source, chosen, slot_of) = refs[18:32]
+    (small_sems, big_sems, weight_sems, row_sems, n_sems, meta_sem) = refs[32:]
     _, channels, width = latent.shape
-    hidden = weight.shape[1]
     samples = frames.shape[0]
     share = block_x.shape[0] * 2
     total = peers * per_pair
@@ -116,13 +74,14 @@
     big = [
         pltpu.make_async_copy(embed_h, embed, big_sems.at[0]),
         pltpu.make_async_copy(gain_h, gain, big_sems.at[1]),
-        pltpu.make_async_copy(head_h, out.at[pl.ds(channels, channels)], big_sems.at[2]),
+        pltpu.make_async_copy(latent, blocks, big_sems.at[2]),
+        pltpu.make_async_copy(head_h, out.at[pl.ds(channels, channels)], big_sems.at[3]),
     ]
     parts = [
-        pltpu.make_async_copy(weight.at[:, pl.ds(n, step)], held.at[:, pl.ds(n, step)], weight_sems.at[n // step])
-        for n in range(0, hidden, step)
+        pltpu.make_async_copy(weight.at[pl.ds(n, step)], held.at[pl.ds(n, step)], weight_sems.at[n // step])
+        for n in range(0, weight.shape[0], step)
     ]
-    for copy in small + big[:2] + parts + big[2:]:
+    for copy in small + big[:3] + parts + big[3:]:
         copy.start()
 
     me = lax.axis_index("mp")
@@ -135,7 +94,7 @@
     for j in range(share + 1):
         chosen[j] = 0
         slot_of[j] = 0
-    for copy in small:
+    for copy in small + big[:3]:
         copy.wait()
     seen = jnp.int32(0)
     count = jnp.int32(0)
@@ -148,8 +107,8 @@
             place = places[o]
             places[o] = place + 1
             q = part_of(place, mp)
-            sends = live & (rest_of(place, mp) == shift) & (q < per_pair)
-            n = jnp.where(sends, o * per_pair + q, total)
+            goes = live & (rest_of(place, mp) == shift) & (q < per_pair)
+            n = jnp.where(goes, o * per_pair + q, total)
             rows[n] = offsets[i] + 1
             source[n] = i
             chosen[count] = s
@@ -160,20 +119,23 @@
 
     copies = [
         pltpu.make_async_copy(
-            latent.at[source[o * per_pair + q]],
-            packed.at[o, pl.ds(q * channels, channels)],
+            blocks.at[source[o * per_pair + q]],
+            send.at[o, pl.ds(q * channels, channels)],
             row_sems.at[o * per_pair + q],
         )
         for o in range(peers)
         for q in range(per_pair)
     ]
     for j in range(share):
-        lanes = pl.ds(j % 2 * width, width)
-        copies.append(pltpu.make_async_copy(latent.at[slot_of[j]], block_x.at[j // 2, :, lanes], x_sems.at[j]))
-        copies.append(pltpu.make_async_copy(noise.at[slot_of[j]], block_n.at[j // 2, :, lanes], n_sems.at[j]))
+        copies.append(
+            pltpu.make_async_copy(
+                noise.at[slot_of[j]], block_n.at[j // 2, :, pl.ds(j % 2 * width, width)], n_sems.at[j]
+            )
+        )
     for copy in copies:
         copy.start()
-    leave = pltpu.make_async_copy(packed, send, leave_sem)
+    for j in range(share):
+        block_x[j // 2, :, j % 2 * width : (j % 2 + 1) * width] = blocks[slot_of[j]]
 
     sub = lax.broadcasted_iota(jnp.int32, picks.shape, 0)
     found = jnp.full(picks.shape, -1, jnp.int32)
@@ -193,29 +155,23 @@
     shared = jnp.where(sub == 4, group, shared)
     for o in range(peers):
         first = lane_row(lambda q: rows[o * per_pair + q].astype(F32), per_pair, F32)
-        packed[o, pl.ds(per_pair * channels, META), :] = jnp.where(sub == 0, first, shared).astype(BF16)
-
-    big[0].wait()
-    e = embed[...]
-    big[1].wait()
-    scaled = e.astype(F32) * gain[...]
+        meta[o] = jnp.where(sub == 0, first, shared).astype(BF16)
+    copies.append(pltpu.make_async_copy(meta, send.at[:, pl.ds(per_pair * channels, META)], meta_sem))
+    copies[-1].start()
+
+    scaled = embed[...].astype(F32) * gain[...]
     hi = scaled.astype(BF16)
     lo = (scaled - hi.astype(F32)).astype(BF16)
     both = jnp.concatenate([hi, lo], axis=0)
+    total_m = None
     for n, copy in enumerate(parts):
         copy.wait()
-        m = jnp.dot(both, held[:, n * step : (n + 1) * step], preferred_element_type=F32)
-        out[:channels, n * step : (n + 1) * step] = (m[:channels] + m[channels:]).astype(BF16)
-        if n == 0:
-            for one in copies[:total]:
-                one.wait()
-            leave.start()
-    hi, mid, lo = split3(lax.dot_general(e, e, (((1,), (1,)), ((), ())), preferred_element_type=F32))
-    gram[...] = jnp.concatenate([hi, mid, lo], axis=0)
-    big[2].wait()
-    for copy in copies[total:]:
+        part = slice(n * step, (n + 1) * step)
+        m = jnp.dot(both[:, part], held[part, :], preferred_element_type=F32)
+        total_m = m if total_m is None else total_m + m
+    out[:channels, :] = (total_m[:channels] + total_m[channels:]).astype(BF16)
+    for copy in big[3:] + copies:
         copy.wait()
-    leave.wait()
 
 
 def norm_factors(xs, gram, features):
@@ -260,8 +216,11 @@
     return [(mt, head, m * hidden) for m, head in enumerate(heads)]
 
 
-def early_kernel(near, features, block_x, gram, *refs):
-    heads, (partial, halves, mt) = refs[:near], refs[near:]
+def early_kernel(near, features, block_x, embed, *refs):
+    heads, (partial, halves, mt, gram) = refs[:near], refs[near:]
+    e = embed[...]
+    hi, mid, lo = split3(lax.dot_general(e, e, (((1,), (1,)), ((), ())), preferred_element_type=F32))
+    gram[...] = jnp.concatenate([hi, mid, lo], axis=0)
     turn(mt, heads)
     xs = [block_x[p] for p in range(block_x.shape[0])]
     half = norm_factors(xs, gram[...], features)
@@ -437,16 +396,16 @@
     share = (slots + 2 * mp - 1) // (2 * mp)
     owner_rows = 3 * samples
     params = functools.partial(pltpu.CompilerParams, vmem_limit_bytes=48 * 1024 * 1024)
-    step = next(n for n in (256, 128, hidden) if hidden % n == 0)
-
-    combined, gram, send, block_x, block_n, picks, info = pl.pallas_call(
-        functools.partial(start_kernel, maxb, per_pair, mp, step),
+    step = next(features // n for n in (3, 2, 1) if features % (128 * n) == 0 or n == 1)
+
+    send, combined, embed, block_x, block_n, picks, info = pl.pallas_call(
+        functools.partial(start_kernel, maxb, per_pair, peers, mp, step),
         in_specs=[HBM] * 11,
-        out_specs=[VMEM] * 2 + [ANY] + [VMEM] * 4,
+        out_specs=[ANY] + [VMEM] * 6,
         out_shape=[
+            jax.ShapeDtypeStruct((peers, per_pair * channels + META, width), BF16),
             jax.ShapeDtypeStruct((2 * channels, hidden), BF16),
-            jax.ShapeDtypeStruct((3 * channels, channels), BF16),
-            jax.ShapeDtypeStruct((peers, per_pair * channels + META, width), BF16),
+            jax.ShapeDtypeStruct((channels, features), BF16),
             jax.ShapeDtypeStruct((share, channels, 2 * width), BF16),
             jax.ShapeDtypeStruct((share, channels, 2 * width), BF16),
             jax.ShapeDtypeStruct((2 * share, LANES), jnp.int32),
@@ -458,20 +417,19 @@
             pltpu.SMEM((slots,), jnp.int32),
             pltpu.SMEM((samples,), jnp.int32),
             pltpu.SMEM((samples,), F32),
-            pltpu.VMEM((channels, features), BF16),
             pltpu.VMEM((1, features), F32),
             pltpu.VMEM((features, hidden), BF16),
-            pltpu.VMEM((peers, per_pair * channels + META, width), BF16),
+            pltpu.VMEM((slots, channels, width), BF16),
+            pltpu.VMEM((peers, META, width), BF16),
             pltpu.SMEM((peers + 1,), jnp.int32),
             pltpu.SMEM((total + 1,), jnp.int32),
             pltpu.SMEM((total + 1,), jnp.int32),
             pltpu.SMEM((2 * share + 1,), jnp.int32),
             pltpu.SMEM((2 * share + 1,), jnp.int32),
             pltpu.SemaphoreType.DMA((5,)),
-            pltpu.SemaphoreType.DMA((3,)),
-            pltpu.SemaphoreType.DMA((hidden // step,)),
+            pltpu.SemaphoreType.DMA((4,)),
+            pltpu.SemaphoreType.DMA((features // step,)),
             pltpu.SemaphoreType.DMA((total,)),
-            pltpu.SemaphoreType.DMA((2 * share,)),
             pltpu.SemaphoreType.DMA((2 * share,)),
             pltpu.SemaphoreType.DMA,
         ],
@@ -496,30 +454,28 @@
         )
     )
 
-    heads = [combined]
-    near = mp
-    while near > 1:
-        near //= 2
-        route = [(j, j ^ near) for j in range(mp)]
-        more = []
-        for head in heads:
-            more.append(lax.ppermute(head, "mp", route))
-        heads += more
-    near = max(mp // 2, 1)
+    def swapped(value, axis, count, bit):
+        return lax.ppermute(value, axis, [(j, j ^ bit) for j in range(count)])
+
     recv = lax.all_to_all(send, "dp", split_axis=0, concat_axis=0, tiled=True)
-
-    partial, halves, mt_near = pl.pallas_call(
+    heads = [combined, swapped(combined, "mp", mp, mp // 2)]
+    for n in range(1, mp // 2):
+        heads += [swapped(head, "mp", mp, n) for head in heads[:2]]
+    near = 2
+
+    partial, halves, mt_near, gram = pl.pallas_call(
         functools.partial(early_kernel, near, features),
         in_specs=[VMEM] * (2 + near),
-        out_specs=[VMEM] * 3,
+        out_specs=[VMEM] * 4,
         out_shape=[
             jax.ShapeDtypeStruct((share, channels, 2 * width), F32),
             jax.ShapeDtypeStruct((share, 1, 2 * width), F32),
             jax.ShapeDtypeStruct((near * hidden, channels), BF16),
+            jax.ShapeDtypeStruct((3 * channels, channels), BF16),
         ],
         compiler_params=params(),
         name="early",
-    )(block_x, gram, *heads[:near])
+    )(block_x, embed, *heads[:near])
 
     errs, mt_far = pl.pallas_call(
         functools.partial(errors_kernel, mp - near),
@@ -580,10 +536,6 @@
         P(None, "mp"),
         P("mp", None),
     )
-    mp = mesh.shape["mp"]
-    near = mp
-    while near > 1:
-        near //= 2
     return jax.shard_map(
         local,
         mesh=mesh,

time: 31.8 us -> 31.1 us (0.978)
  Pallas kernels: 11 us -> 10.6 us
    pallas_call x1, Pallas kernels: 4.15 us -> 3.45 us  [local(): pl.pallas_call(functools.partial(start_kernel, maxb, per_pair, peers, mp,...]
  transfers between devices with their start and end apart: 4 -> 4, of which waited for: 1 -> 1; matrix products, arithmetic and copies ran while one was open for 0% -> 0% of each run, Pallas kernels for 12% -> 13%
where the time goes in v3:
time: 31.1 us; the launch traced here: 30.8 us
  Pallas kernels  10.6 us (34%)
  starting transfers between devices  9.36 us (30%)
  blocking collectives  7.16 us (23%)
  waiting for transfers between devices  2.83 us (9%)
  between operations  0.84 us (3%)
    all_gather x1, blocking collectives, local(): gathered = lax.all_gather(payload, 'mp', axis=0, tiled=False)  7.16 us
    all_to_all x1, starting transfers between devices, local(): recv = lax.all_to_all(send, 'dp', split_axis=0, concat_axis=0, tiled=True)  5.84 us
    ppermute x3, starting transfers between devices, swapped(): return lax.ppermute(value, axis, [(j, j ^ bit) for j in range(count)])  3.53 us
    pallas_call x1, Pallas kernels, local(): pl.pallas_call(functools.partial(start_kernel, maxb, per_pair, peers, mp,...  3.45 us
    all_to_all x1, waiting for transfers between devices, local(): recv = lax.all_to_all(send, 'dp', split_axis=0, concat_axis=0, tiled=True)  2.81 us
    pallas_call x1, Pallas kernels, local(): pl.pallas_call(functools.partial(early_kernel, near, features), in_specs=...  2.3 us
    pallas_call x1, Pallas kernels, local(): pl.pallas_call(functools.partial(owner_kernel, per_pair, near, mp, featur...  2.14 us
    pallas_call x1, Pallas kernels, local(): pl.pallas_call(functools.partial(errors_kernel, mp - near), in_specs=[VME...  1.79 us
  transfers between devices with their start and end apart: 4, of which 1 were waited for; matrix products, arithmetic and copies ran while one was open for 0% of the time, Pallas kernels for 13%

profile of v3, /device:TPU:0, one launch (start us, length us, event | category | flops | bytes accessed | tf_op | source)
XLA Modules:
  0.0 30.8 jit_solution(6022871987083460962)
XLA Ops:
  0.6 3.4 %start.1 = (bf16[8,72,128]{2,1,0:T(8,128)(2,1)}, bf16[128,768]{1,0:T(8,128)(2,1)S(1)}, bf16[64,3072]{1,0:T(8,128)(2,1)S(1)}, bf16[4,64,256]{2,1,0:T(8,128)(2,1)S...) custom-call(s32[6]{0:T(128)} %refs_0_.1, s32[30]{0:T(128)} %refs_1_.1, ...), custom_call_target="tpu_custom_call" | custom-call | tf_op jit(solution)/shard_map/start/pallas_call | solution.py:401
  4.1 3.0 %collective-permute-start = (bf16[128,768]{1,0:T(8,128)(2,1)S(1)}, bf16[128,768]{1,0:T(8,128)(2,1)S(1)}, u32[]{:S(2)}, u32[]{:S(2)}) collective-permute-start(bf16[128,768]{1,0:T(8,128)(2,1)S(1)} %get-tuple-element.22.refs_0_), channel_id=1, source_target_pairs={{0,2},{1,3},{2,0},{3,1},{4,6},{5,7},{6,4},{7,5},{8,10},{9,11},{10,... | collective-permute-start | bytes 589832 | tf_op jit(solution)/shard_map/ppermute | solution.py:458
  7.1 5.8 %all-to-all-start = ((bf16[8,72,128]{2,1,0:T(8,128)(2,1)}), bf16[8,72,128]{2,1,0:T(8,128)(2,1)S(1)}, u32[]{:S(2)}, u32[]{:S(2)}) async-start(bf16[8,72,128]{2,1,0:T(8,128)(2,1)} %get-tuple-element.17), calls=%async_computation | async-start | bytes 294912 | tf_op jit(solution)/shard_map/all_to_all | solution.py:460
  13.0 0.0 collective-permute-start.1
  13.0 0.0 collective-permute-done.refs_1_
  13.0 0.5 %collective-permute-start.2 = (bf16[128,768]{1,0:T(8,128)(2,1)S(1)}, bf16[128,768]{1,0:T(8,128)(2,1)S(1)}, u32[]{:S(2)}, u32[]{:S(2)}) collective-permute-start(bf16[128,768]{1,0:T(8,128)(2,1)S(1)} %collective-permute-done.refs_1_), channel_id=1, source_target_pairs={{0,1},{1,0},{2,3},{3,2},{4,5},{5,4},{6,7},{7,6},{8,9},{9,8},{10,11... | collective-permute-start | bytes 589832 | tf_op jit(solution)/shard_map/ppermute | solution.py:458
  13.5 2.3 %early.1 = (f32[4,64,256]{2,1,0:T(8,128)S(1)}, f32[4,1,256]{2,1,0:T(1,128)S(1)}, bf16[1536,64]{1,0:T(8,128)(2,1)S(1)}, bf16[192,64]{1,0:T(8,128)(2,1)S(1)}) custom-call(bf16[4,64,256]{2,1,0:T(8,128)(2,1)S(1)} %get-tuple-element.19.block_x, bf16[64,3072]{1,0:T(8,128)(2,1)S(1)} %get-tuple-element.21.embed, bf16[128,768]{1,0:T(8,128)(2,1)S(1)} %get-tuple-element.22.refs_0_, ...), custom_call_target="tpu_custom_call" | custom-call | tf_op jit(solution)/shard_map/early/pallas_call | solution.py:466
  15.8 0.0 collective-permute-done.1.refs_0_.refs_2_
  15.8 0.0 collective-permute-done.2.refs_1_.refs_3_
  15.8 1.8 %errors.1 = (f32[1,128]{1,0:T(1,128)S(1)}, bf16[1536,64]{1,0:T(8,128)(2,1)S(1)}) custom-call(s32[8,128]{1,0:T(8,128)S(1)} %get-tuple-element.18.picks, bf16[4,64,256]{2,1,0:T(8,128)(2,1)S(1)} %get-tuple-element.19.block_x, bf16[4,64,256]{2,1,0:T(8,128)(2,1)S(1)} %get-tuple-element.20.block_n, f32[4,64,256]{2,1,0:T(8,128)S(1)} %get-tuple-element.23.partial, ...), custom_call_target="tpu_custom_call" | custom-call | tf_op jit(solution)/shard_map/errors/pallas_call | solution.py:480
  17.6 2.8 %all-to-all-done.recv = bf16[8,72,128]{2,1,0:T(8,128)(2,1)S(1)} async-done(((bf16[8,72,128]{2,1,0:T(8,128)(2,1)}), bf16[8,72,128]{2,1,0:T(8,128)(2,1)S(1)}, u32[]{:S(2)}, u32[]{:S(2)}) %all-to-all-start) | async-done | bytes 147488 | tf_op jit(solution)/shard_map/all_to_all | solution.py:460
  20.4 2.1 %owner.1 = bf16[528,128]{1,0:T(8,128)(2,1)S(1)} custom-call(bf16[8,72,128]{2,1,0:T(8,128)(2,1)S(1)} %all-to-all-done.recv, f32[1,128]{1,0:T(1,128)S(1)} %get-tuple-element.25.errs, bf16[192,64]{1,0:T(8,128)(2,1)S(1)} %get-tuple-element.26.gram, bf16[1536,64]{1,0:T(8,128)(2,1)S(1)} %get-tuple-element.27.mt_near, ...), custom_call_target="tpu_custom_call" | custom-call | tf_op jit(solution)/shard_map/owner/pallas_call | solution.py:493
  22.6 7.2 %all-gather = bf16[2112,128]{1,0:T(8,128)(2,1)S(1)} all-gather(bf16[528,128]{1,0:T(8,128)(2,1)S(1)} %owner.1), channel_id=2, replica_groups=mesh['dp'=8,'mp'=4] {'mp'}, dimensions={0}, use_global_device_ids=true | all-gather | bytes 675840 | tf_op jit(solution)/shard_map/all_gather | solution.py:503
  29.7 1.0 %place.1 = (bf16[18,64,128]{2,1,0:T(8,128)(2,1)}, f32[6]{0:T(128)}, f32[6]{0:T(128)}) custom-call(f32[8,128]{1,0:T(8,128)S(1)} %get-tuple-element.16.info, bf16[8,72,128]{2,1,0:T(8,128)(2,1)S(1)} %all-to-all-done.recv, bf16[4,528,128]{2,1,0:T(8,128)(2,1)S(1)} %bitcast.3), custom_call_target="tpu_custom_call" | custom-call | tf_op jit(solution)/shard_map/place/pallas_call | solution.py:505
Async XLA Ops:
  4.1 8.9 %collective-permute-start = (bf16[128,768]{1,0:T(8,128)(2,1)S(1)}, bf16[128,768]{1,0:T(8,128)(2,1)S(1)}, u32[]{:S(2)}, u32[]{:S(2)}) collective-permute-start(bf16[128,768]{1,0:T(8,128)(2,1)S(1)} %get-tuple-element.22.refs_0_), channel_id=1, source_target_pairs={{0,2},{1,3},{2,0},{3,1},{4,6},{5,7},{6,4},{7,5},{8,10},{9,11},{10,... | collective-permute-start | bytes 589832 | tf_op jit(solution)/shard_map/ppermute | solution.py:458
  7.1 13.3 %all-to-all-start = ((bf16[8,72,128]{2,1,0:T(8,128)(2,1)}), bf16[8,72,128]{2,1,0:T(8,128)(2,1)S(1)}, u32[]{:S(2)}, u32[]{:S(2)}) async-start(bf16[8,72,128]{2,1,0:T(8,128)(2,1)} %get-tuple-element.17), calls=%async_computation | async-start | bytes 294912 | tf_op jit(solution)/shard_map/all_to_all | solution.py:460
  13.0 2.8 %collective-permute-start.1 = (bf16[128,768]{1,0:T(8,128)(2,1)S(1)}, bf16[128,768]{1,0:T(8,128)(2,1)S(1)}, u32[]{:S(2)}, u32[]{:S(2)}) collective-permute-start(bf16[128,768]{1,0:T(8,128)(2,1)S(1)} %get-tuple-element.22.refs_0_), channel_id=1, source_target_pairs={{0,1},{1,0},{2,3},{3,2},{4,5},{5,4},{6,7},{7,6},{8,9},{9,8},{10,11... | collective-permute-start | bytes 589832 | tf_op jit(solution)/shard_map/ppermute | solution.py:458
  13.0 2.8 %collective-permute-start.2 = (bf16[128,768]{1,0:T(8,128)(2,1)S(1)}, bf16[128,768]{1,0:T(8,128)(2,1)S(1)}, u32[]{:S(2)}, u32[]{:S(2)}) collective-permute-start(bf16[128,768]{1,0:T(8,128)(2,1)S(1)} %collective-permute-done.refs_1_), channel_id=1, source_target_pairs={{0,1},{1,0},{2,3},{3,2},{4,5},{5,4},{6,7},{7,6},{8,9},{9,8},{10,11... | collective-permute-start | bytes 589832 | tf_op jit(solution)/shard_map/ppermute | solution.py:458

commit v4 on v3

--- a/solution.py
+++ b/solution.py
@@ -194,12 +194,15 @@
         totals[p] = part if totals[p] is None else totals[p] + part
 
     for p, x in enumerate(xs):
+        exact = x.astype(F32) * halves[p]
+        hi = exact.astype(BF16)
+        lo = (exact - hi.astype(F32)).astype(BF16)
+        x = jnp.concatenate([hi, lo], axis=0)
         for mt, both, row in parts:
             channels, hidden = both.shape[0] // 2, both.shape[1]
-            mid = jnp.dot(mt[row : row + hidden, :], x, preferred_element_type=F32)
+            v = jnp.dot(mt[row : row + hidden, :], x, preferred_element_type=F32)
             if waiting:
                 finish()
-            v = mid * halves[p]
             waiting.append((p, both[channels:, :], (v + v * jnp.tanh(v)).astype(BF16)))
     finish()
     return totals
@@ -208,7 +211,7 @@
 def turn(mt, heads):
     channels, hidden = heads[0].shape[0] // 2, heads[0].shape[1]
     for m, head in enumerate(heads):
-        mt[m * hidden : (m + 1) * hidden, :] = head[:channels, :].T
+        mt[m * hidden : (m + 1) * hidden, :] = jnp.concatenate([head[:channels, :]] * 2, axis=0).T
 
 
 def shards_of(mt, heads):
@@ -470,7 +473,7 @@
         out_shape=[
             jax.ShapeDtypeStruct((share, channels, 2 * width), F32),
             jax.ShapeDtypeStruct((share, 1, 2 * width), F32),
-            jax.ShapeDtypeStruct((near * hidden, channels), BF16),
+            jax.ShapeDtypeStruct((near * hidden, 2 * channels), BF16),
             jax.ShapeDtypeStruct((3 * channels, channels), BF16),
         ],
         compiler_params=params(),
@@ -483,7 +486,7 @@
         out_specs=[VMEM, VMEM],
         out_shape=[
             jax.ShapeDtypeStruct((1, LANES), F32),
-            jax.ShapeDtypeStruct(((mp - near) * hidden, channels), BF16),
+            jax.ShapeDtypeStruct(((mp - near) * hidden, 2 * channels), BF16),
         ],
         compiler_params=params(),
         name="errors",

time: 31.1 us -> 31 us (level)
  no operation moved by 1% of the time
where the time goes in v4:
time: 31 us; the launch traced here: 30.8 us
  Pallas kernels  10.6 us (34%)
  starting transfers between devices  9.36 us (30%)
  blocking collectives  7.03 us (23%)
  waiting for transfers between devices  2.91 us (9%)
  between operations  0.84 us (3%)
    all_gather x1, blocking collectives, local(): gathered = lax.all_gather(payload, 'mp', axis=0, tiled=False)  7.03 us
    all_to_all x1, starting transfers between devices, local(): recv = lax.all_to_all(send, 'dp', split_axis=0, concat_axis=0, tiled=True)  5.84 us
    ppermute x3, starting transfers between devices, swapped(): return lax.ppermute(value, axis, [(j, j ^ bit) for j in range(count)])  3.53 us
    pallas_call x1, Pallas kernels, local(): pl.pallas_call(functools.partial(start_kernel, maxb, per_pair, peers, mp,...  3.45 us
    all_to_all x1, waiting for transfers between devices, local(): recv = lax.all_to_all(send, 'dp', split_axis=0, concat_axis=0, tiled=True)  2.89 us
    pallas_call x1, Pallas kernels, local(): pl.pallas_call(functools.partial(early_kernel, near, features), in_specs=...  2.26 us
    pallas_call x1, Pallas kernels, local(): pl.pallas_call(functools.partial(owner_kernel, per_pair, near, mp, featur...  2.18 us
    pallas_call x1, Pallas kernels, local(): pl.pallas_call(functools.partial(errors_kernel, mp - near), in_specs=[VME...  1.76 us
  transfers between devices with their start and end apart: 4, of which 1 were waited for; matrix products, arithmetic and copies ran while one was open for 0% of the time, Pallas kernels for 13%

profile of v4, /device:TPU:0, one launch (start us, length us, event | category | flops | bytes accessed | tf_op | source)
XLA Modules:
  0.0 30.8 jit_solution(3965229243813715243)
XLA Ops:
  0.6 3.4 %start.1 = (bf16[8,72,128]{2,1,0:T(8,128)(2,1)}, bf16[128,768]{1,0:T(8,128)(2,1)S(1)}, bf16[64,3072]{1,0:T(8,128)(2,1)S(1)}, bf16[4,64,256]{2,1,0:T(8,128)(2,1)S...) custom-call(s32[6]{0:T(128)} %refs_0_.1, s32[30]{0:T(128)} %refs_1_.1, ...), custom_call_target="tpu_custom_call" | custom-call | tf_op jit(solution)/shard_map/start/pallas_call | solution.py:404
  4.1 3.0 %collective-permute-start = (bf16[128,768]{1,0:T(8,128)(2,1)S(1)}, bf16[128,768]{1,0:T(8,128)(2,1)S(1)}, u32[]{:S(2)}, u32[]{:S(2)}) collective-permute-start(bf16[128,768]{1,0:T(8,128)(2,1)S(1)} %get-tuple-element.22.refs_0_), channel_id=1, source_target_pairs={{0,2},{1,3},{2,0},{3,1},{4,6},{5,7},{6,4},{7,5},{8,10},{9,11},{10,... | collective-permute-start | bytes 589832 | tf_op jit(solution)/shard_map/ppermute | solution.py:461
  7.1 5.8 %all-to-all-start = ((bf16[8,72,128]{2,1,0:T(8,128)(2,1)}), bf16[8,72,128]{2,1,0:T(8,128)(2,1)S(1)}, u32[]{:S(2)}, u32[]{:S(2)}) async-start(bf16[8,72,128]{2,1,0:T(8,128)(2,1)} %get-tuple-element.17), calls=%async_computation | async-start | bytes 294912 | tf_op jit(solution)/shard_map/all_to_all | solution.py:463
  13.0 0.0 collective-permute-start.1
  13.0 0.0 collective-permute-done.refs_1_
  13.0 0.5 %collective-permute-start.2 = (bf16[128,768]{1,0:T(8,128)(2,1)S(1)}, bf16[128,768]{1,0:T(8,128)(2,1)S(1)}, u32[]{:S(2)}, u32[]{:S(2)}) collective-permute-start(bf16[128,768]{1,0:T(8,128)(2,1)S(1)} %collective-permute-done.refs_1_), channel_id=1, source_target_pairs={{0,1},{1,0},{2,3},{3,2},{4,5},{5,4},{6,7},{7,6},{8,9},{9,8},{10,11... | collective-permute-start | bytes 589832 | tf_op jit(solution)/shard_map/ppermute | solution.py:461
  13.5 2.3 %early.1 = (f32[4,64,256]{2,1,0:T(8,128)S(1)}, f32[4,1,256]{2,1,0:T(1,128)S(1)}, bf16[1536,128]{1,0:T(8,128)(2,1)S(1)}, bf16[192,64]{1,0:T(8,128)(2,1)S(1)}) custom-call(bf16[4,64,256]{2,1,0:T(8,128)(2,1)S(1)} %get-tuple-element.19.block_x, bf16[64,3072]{1,0:T(8,128)(2,1)S(1)} %get-tuple-element.21.embed, bf16[128,768]{1,0:T(8,128)(2,1)S(1)} %get-tuple-element.22.refs_0_, ...), custom_call_target="tpu_custom_call" | custom-call | tf_op jit(solution)/shard_map/early/pallas_call | solution.py:469
  15.7 0.0 collective-permute-done.1.refs_0_.refs_2_
  15.8 0.0 collective-permute-done.2.refs_1_.refs_3_
  15.8 1.8 %errors.1 = (f32[1,128]{1,0:T(1,128)S(1)}, bf16[1536,128]{1,0:T(8,128)(2,1)S(1)}) custom-call(s32[8,128]{1,0:T(8,128)S(1)} %get-tuple-element.18.picks, bf16[4,64,256]{2,1,0:T(8,128)(2,1)S(1)} %get-tuple-element.19.block_x, bf16[4,64,256]{2,1,0:T(8,128)(2,1)S(1)} %get-tuple-element.20.block_n, f32[4,64,256]{2,1,0:T(8,128)S(1)} %get-tuple-element.23.partial, ...), custom_call_target="tpu_custom_call" | custom-call | tf_op jit(solution)/shard_map/errors/pallas_call | solution.py:483
  17.5 2.9 %all-to-all-done.recv = bf16[8,72,128]{2,1,0:T(8,128)(2,1)S(1)} async-done(((bf16[8,72,128]{2,1,0:T(8,128)(2,1)}), bf16[8,72,128]{2,1,0:T(8,128)(2,1)S(1)}, u32[]{:S(2)}, u32[]{:S(2)}) %all-to-all-start) | async-done | bytes 147488 | tf_op jit(solution)/shard_map/all_to_all | solution.py:463
  20.4 2.2 %owner.1 = bf16[528,128]{1,0:T(8,128)(2,1)S(1)} custom-call(bf16[8,72,128]{2,1,0:T(8,128)(2,1)S(1)} %all-to-all-done.recv, f32[1,128]{1,0:T(1,128)S(1)} %get-tuple-element.25.errs, bf16[192,64]{1,0:T(8,128)(2,1)S(1)} %get-tuple-element.26.gram, bf16[1536,128]{1,0:T(8,128)(2,1)S(1)} %get-tuple-element.27.mt_near, ...), custom_call_target="tpu_custom_call" | custom-call | tf_op jit(solution)/shard_map/owner/pallas_call | solution.py:496
  22.6 7.0 %all-gather = bf16[2112,128]{1,0:T(8,128)(2,1)S(1)} all-gather(bf16[528,128]{1,0:T(8,128)(2,1)S(1)} %owner.1), channel_id=2, replica_groups=mesh['dp'=8,'mp'=4] {'mp'}, dimensions={0}, use_global_device_ids=true | all-gather | bytes 675840 | tf_op jit(solution)/shard_map/all_gather | solution.py:506
  29.6 1.0 %place.1 = (bf16[18,64,128]{2,1,0:T(8,128)(2,1)}, f32[6]{0:T(128)}, f32[6]{0:T(128)}) custom-call(f32[8,128]{1,0:T(8,128)S(1)} %get-tuple-element.16.info, bf16[8,72,128]{2,1,0:T(8,128)(2,1)S(1)} %all-to-all-done.recv, bf16[4,528,128]{2,1,0:T(8,128)(2,1)S(1)} %bitcast.3), custom_call_target="tpu_custom_call" | custom-call | tf_op jit(solution)/shard_map/place/pallas_call | solution.py:508
Async XLA Ops:
  4.1 8.9 %collective-permute-start = (bf16[128,768]{1,0:T(8,128)(2,1)S(1)}, bf16[128,768]{1,0:T(8,128)(2,1)S(1)}, u32[]{:S(2)}, u32[]{:S(2)}) collective-permute-start(bf16[128,768]{1,0:T(8,128)(2,1)S(1)} %get-tuple-element.22.refs_0_), channel_id=1, source_target_pairs={{0,2},{1,3},{2,0},{3,1},{4,6},{5,7},{6,4},{7,5},{8,10},{9,11},{10,... | collective-permute-start | bytes 589832 | tf_op jit(solution)/shard_map/ppermute | solution.py:461
  7.1 13.3 %all-to-all-start = ((bf16[8,72,128]{2,1,0:T(8,128)(2,1)}), bf16[8,72,128]{2,1,0:T(8,128)(2,1)S(1)}, u32[]{:S(2)}, u32[]{:S(2)}) async-start(bf16[8,72,128]{2,1,0:T(8,128)(2,1)} %get-tuple-element.17), calls=%async_computation | async-start | bytes 294912 | tf_op jit(solution)/shard_map/all_to_all | solution.py:463
  13.0 2.8 %collective-permute-start.1 = (bf16[128,768]{1,0:T(8,128)(2,1)S(1)}, bf16[128,768]{1,0:T(8,128)(2,1)S(1)}, u32[]{:S(2)}, u32[]{:S(2)}) collective-permute-start(bf16[128,768]{1,0:T(8,128)(2,1)S(1)} %get-tuple-element.22.refs_0_), channel_id=1, source_target_pairs={{0,1},{1,0},{2,3},{3,2},{4,5},{5,4},{6,7},{7,6},{8,9},{9,8},{10,11... | collective-permute-start | bytes 589832 | tf_op jit(solution)/shard_map/ppermute | solution.py:461
  13.0 2.8 %collective-permute-start.2 = (bf16[128,768]{1,0:T(8,128)(2,1)S(1)}, bf16[128,768]{1,0:T(8,128)(2,1)S(1)}, u32[]{:S(2)}, u32[]{:S(2)}) collective-permute-start(bf16[128,768]{1,0:T(8,128)(2,1)S(1)} %collective-permute-done.refs_1_), channel_id=1, source_target_pairs={{0,1},{1,0},{2,3},{3,2},{4,5},{5,4},{6,7},{7,6},{8,9},{9,8},{10,11... | collective-permute-start | bytes 589832 | tf_op jit(solution)/shard_map/ppermute | solution.py:461
